TPU v7x, 128 devices: a whole 4x4x4 slice. The times are simulated.
128 devices in a mesh: lat: 16 (over z_lo, y, core), lon: 8 (over z_hi, x).
Axes of the slice: x: 4, y: 4, z: 4 (z_hi: 2, z_lo: 2; z = z_hi * 2 + z_lo), core: 2. Of those that a mesh axis runs over, the one named last changes fastest.
Arguments:
- tokens: bfloat16 [4, 128, 256, 1024], P(None, 'lat', 'lon'), may hold values from -6 to 6
- qkv_weight: bfloat16 [3072, 1024], P(('lat', 'lon')), may hold values from -0.1875 to 0.1875
- proj_weight: bfloat16 [1024, 1024], P(('lat', 'lon')), may hold values from -0.1875 to 0.1875
- up_weight: bfloat16 [4096, 1024], P(('lat', 'lon')), may hold values from -0.1875 to 0.1875
- down_weight: bfloat16 [4096, 1024], P(('lat', 'lon')), may hold values from -0.09375 to 0.09375
- bias_table: float32 [225, 16], replicated, may hold values from -3 to 220
- sea_mask: int32 [128, 256], replicated, may hold values 0 or 1
Outputs:
- block_out: bfloat16 [4, 128, 256, 1024], P(None, 'lat', 'lon')
All inputs are finite; a program needn't handle non-finite values.
Results may differ from a plain program's by a relative error of at most 0.012.
Values may be sent and summed in bfloat16 or wider, within the bound.
A program may use at most 128 MiB of HBM per device.

v0:
```python
import jax
import jax.numpy as jnp
from jax import lax
from jax.sharding import PartitionSpec as P


def from_behind(value, axis, steps):
    count = lax.axis_size(axis)
    pairs = [(source, (source + steps) % count) for source in range(count)]
    return lax.ppermute(value, axis, pairs)


def sent_together(arrays, axis, dim, along):
    ends, at = ([], 0)
    for a in arrays[:-1]:
        at += a.shape[along]
        ends.append(at)
    both = jnp.concatenate(arrays, axis=along)
    return tuple(jnp.split(lax.all_gather(both, axis, axis=dim, tiled=True), ends, axis=along))


def layer_norm(values):
    widened = values.astype(jnp.float32)
    centre = jnp.mean(widened, axis=-1, keepdims=True)
    spread = jnp.mean(jnp.square(widened - centre), axis=-1, keepdims=True)
    return ((widened - centre) * lax.rsqrt(spread + 1e-05)).astype(jnp.bfloat16)


def offsets_table():
    cell_ids = jnp.arange(64, dtype=jnp.int32)
    row_of = cell_ids // 8
    col_of = cell_ids % 8
    return (row_of[:, None] - row_of[None, :] + 7) * 15 + (col_of[:, None] - col_of[None, :] + 7)


def row_region(row_ids, total_rows):
    return jnp.where(row_ids < 4, 2, jnp.where(row_ids >= total_rows - 4, 1, 0)).astype(jnp.int32)


def window_attention(queries, pair_cells, row_start, col_start, sea_mask, pos_bias):
    batch_size, row_count, col_count, feat_width = queries.shape
    head_count = pos_bias.shape[0]
    head_size = feat_width // head_count
    lat_cells, lon_cells = sea_mask.shape
    down_count = row_count // 8
    across_count = col_count // 8
    window_count = down_count * across_count

    def to_windows(values):
        last_dim = values.shape[-1]
        shaped = values.reshape(batch_size, down_count, 8, across_count, 8, last_dim)
        return shaped.transpose(0, 1, 3, 2, 4, 5).reshape(batch_size, window_count, 64, last_dim)

    query_win = to_windows(queries)
    pair_win = to_windows(pair_cells)
    grid_rows = (row_start + jnp.arange(row_count, dtype=jnp.int32)) % lat_cells
    region = row_region(grid_rows, lat_cells).reshape(down_count, 8)
    region = jnp.broadcast_to(region[:, None, :, None], (down_count, across_count, 8, 8)).reshape(
        window_count, 64
    )
    sea_tiled = jnp.tile(sea_mask, (2, 2))
    sea_keep = lax.dynamic_slice(
        sea_tiled, (row_start % lat_cells, col_start % lon_cells), (row_count, col_count)
    )
    sea_keep = (
        sea_keep.reshape(down_count, 8, across_count, 8)
        .transpose(0, 2, 1, 3)
        .reshape(window_count, 64)
        == 1
    )
    same_cell = jnp.eye(64, dtype=bool)
    allowed = (region[:, :, None] == region[:, None, :]) & (sea_keep[:, None, :] | same_cell[None])
    group_width = 4 * head_size
    score_scale = head_size ** (-0.5)

    def one_group(group_index):
        first_col = group_index * group_width
        split_shape = (batch_size, window_count, 64, 4, head_size)
        query_part = lax.dynamic_slice_in_dim(query_win, first_col, group_width, 3).reshape(
            split_shape
        )
        key_part = lax.dynamic_slice_in_dim(pair_win, first_col, group_width, 3).reshape(
            split_shape
        )
        value_part = lax.dynamic_slice_in_dim(
            pair_win, feat_width + first_col, group_width, 3
        ).reshape(split_shape)
        bias_part = lax.dynamic_slice_in_dim(pos_bias, group_index * 4, 4, 0)
        scores = jnp.einsum(
            "bsqhd,bskhd->bshqk", query_part, key_part, preferred_element_type=jnp.float32
        )
        scores = scores * score_scale + bias_part[None, None]
        scores = jnp.where(allowed[None, :, None], scores, -1e30)
        row_top = jnp.max(scores, axis=-1, keepdims=True)
        weights = jnp.exp(scores - row_top)
        attn_probs = (weights / jnp.sum(weights, axis=-1, keepdims=True)).astype(jnp.bfloat16)
        context = jnp.einsum(
            "bshqk,bskhd->bsqhd", attn_probs, value_part, preferred_element_type=jnp.float32
        )
        return context.astype(jnp.bfloat16).reshape(batch_size, window_count, 64, group_width)

    groups = lax.map(one_group, jnp.arange(head_count // 4, dtype=jnp.int32))
    context = jnp.transpose(groups, (1, 2, 3, 0, 4)).reshape(
        batch_size, down_count, across_count, 8, 8, feat_width
    )
    return context.transpose(0, 1, 3, 2, 4, 5).reshape(batch_size, row_count, col_count, feat_width)


def per_device(tokens, qkv_weight, proj_weight, up_weight, down_weight, bias_table, sea_mask):
    batch_size, lat_rows, lon_cols, feat_width = tokens.shape
    head_count = bias_table.shape[1]
    row_base = lax.axis_index("lat") * lat_rows
    col_base = lax.axis_index("lon") * lon_cols
    offset_ids = offsets_table().reshape(-1)
    one_hot = (
        offset_ids[:, None] == jnp.arange(bias_table.shape[0], dtype=jnp.int32)[None, :]
    ).astype(jnp.float32)
    pos_bias = jnp.dot(one_hot, bias_table, precision=lax.Precision.HIGHEST)
    pos_bias = pos_bias.reshape(64, 64, head_count).transpose(2, 0, 1)
    normed = layer_norm(tokens)
    arrived = from_behind(normed[:, :4], "lat", -1)
    rolled_rows = jnp.concatenate([normed[:, 4:], arrived], axis=1)
    arrived_cols = from_behind(rolled_rows[:, :, :4], "lon", -1)
    feed_cells = jnp.concatenate([rolled_rows[:, :, 4:], arrived_cols], axis=2)
    feed_flat = feed_cells.reshape(-1, feat_width)
    projected = lax.dot_general(
        feed_flat,
        lax.all_gather(qkv_weight, ("lat", "lon"), axis=0, tiled=True),
        (((1,), (1,)), ((), ())),
        preferred_element_type=jnp.float32,
    ).astype(jnp.bfloat16)
    projected = projected.reshape(batch_size, lat_rows, lon_cols, 3 * feat_width)
    queries = projected[..., :feat_width]
    pair_cells = projected[..., feat_width:]
    rolled_context = window_attention(
        queries, pair_cells, row_base + 4, col_base + 4, sea_mask, pos_bias
    )
    came_cols = from_behind(rolled_context[:, :, lon_cols - 4 :], "lon", 1)
    back_cols = jnp.concatenate([came_cols, rolled_context[:, :, : lon_cols - 4]], axis=2)
    came_rows = from_behind(back_cols[:, lat_rows - 4 :], "lat", 1)
    context = jnp.concatenate([came_rows, back_cols[:, : lat_rows - 4]], axis=1)
    context_flat = context.reshape(-1, feat_width)
    attention_out = lax.dot_general(
        context_flat,
        lax.all_gather(proj_weight, ("lat", "lon"), axis=0, tiled=True),
        (((1,), (1,)), ((), ())),
        preferred_element_type=jnp.float32,
    )
    attended = (tokens.reshape(-1, feat_width).astype(jnp.float32) + attention_out).astype(
        jnp.bfloat16
    )
    normed_two = layer_norm(attended)
    up_part, down_part = sent_together((up_weight, down_weight), ("lat", "lon"), 0, 1)
    hidden = lax.dot_general(
        normed_two, up_part, (((1,), (1,)), ((), ())), preferred_element_type=jnp.float32
    )
    hidden = jax.nn.gelu(hidden).astype(jnp.bfloat16)
    hidden_sum = jnp.dot(hidden, down_part, preferred_element_type=jnp.float32)
    result = (attended.astype(jnp.float32) + hidden_sum).astype(jnp.bfloat16)
    return result.reshape(tokens.shape)


def solution(mesh):
    placed = (
        P(None, "lat", "lon", None),
        P(("lat", "lon"), None),
        P(("lat", "lon"), None),
        P(("lat", "lon"), None),
        P(("lat", "lon"), None),
        P(),
        P(),
    )
    return jax.shard_map(
        per_device,
        mesh=mesh,
        in_specs=placed,
        out_specs=P(None, "lat", "lon", None),
        check_vma=False,
    )
```

profile of v0, /device:TPU:1, one launch (start us, length us, event | category | flops | bytes accessed | tf_op | source)
XLA Modules:
  0.0 980.6 jit_solution(1794347280123285395)
XLA Ops:
  8.1 1.5 pad_maximum_fusion.3
  9.6 1.9 convert_reduce_fusion.1
  11.6 2.3 multiply_reduce_fusion
  14.5 1.2 fusion.79
  15.6 1.4 collective-permute-start
  17.8 2.6 fusion.48
  20.6 1.0 copy.26
  21.7 9.3 collective-permute-done
  31.1 7.6 collective-permute-start.1
  39.3 4.4 collective-permute-done.1
  44.1 274.7 %all-gather.4.cloned.1.call-done = bf16[3072,1024]{1,0:T(8,128)(2,1)} async-done(((bf16[24,1024]{1,0:T(8,128)(2,1)}), bf16[3072,1024]{1,0:T(8,128)(2,1)}) %all-gather.4.cloned.1.call-update) | async-done | bytes 6291472 | tf_op jit(solution)/shard_map/all_gather | solution.py:128
  318.8 9.7 convolution_convert_fusion.1
  328.5 1.5 copy_bitcast_fusion.2
  330.0 2.3 copy_bitcast_fusion
  332.4 45.6 %while.13 = (s32[]{:T(128)}, bf16[4,4,4,64,256]{3,4,2,1,0:T(8,128)(2,1)}, s32[4]{0:T(128)S(1)}, bf16[4,4,64,2048]{3,2,1,0:T(8,128)(2,1)}, bf16[4,4,64,1024]{3,2,...) while((s32[]{:T(128)}, ...), condition=%wide.region_5.6_spmd.clone, body=%wide.region_2.5_spmd.clone.sunk | while | flops 69255248 | bytes 12326224 | solution.py:102
  333.6 1.5 constant_dynamic-slice_fusion.6
  336.6 0.9 constant_dynamic-slice_fusion.7
  337.6 2.6 fusion.94
  340.7 2.0 convolution_convert_fusion.3
  342.7 1.1 constant_dynamic-update-slice_fusion.2
  345.0 1.5 constant_dynamic-slice_fusion.6
  348.0 0.9 constant_dynamic-slice_fusion.7
  349.0 2.6 fusion.94
  352.1 2.0 convolution_convert_fusion.3
  354.1 1.1 constant_dynamic-update-slice_fusion.2
  356.4 1.5 constant_dynamic-slice_fusion.6
  359.4 0.9 constant_dynamic-slice_fusion.7
  360.4 2.6 fusion.94
  363.5 2.0 convolution_convert_fusion.3
  365.5 1.1 constant_dynamic-update-slice_fusion.2
  367.9 1.5 constant_dynamic-slice_fusion.6
  370.8 0.9 constant_dynamic-slice_fusion.7
  371.8 2.6 fusion.94
  374.9 2.0 convolution_convert_fusion.3
  376.9 1.0 constant_dynamic-update-slice_fusion.2
  378.0 5.5 copy.28
  383.5 2.7 reshape.220
  386.2 1.8 copy_bitcast_fusion.1
  388.2 0.9 collective-permute-start.2
  389.1 10.5 %collective-permute-done.2 = bf16[4,8,4,1024]{3,2,1,0:T(4,128)(2,1)S(1)} collective-permute-done((bf16[4,8,4,1024]{3,2,1,0:T(4,128)(2,1)S(1)}, bf16[4,8,4,1024]{3,2,1,0:T(4,128)(2,1)S(1)}, u32[]{:S(2)}, u32[]{:S(2)}) %collective-permute-start.2) | collective-permute-done | bytes 262176 | tf_op jit(solution)/shard_map/ppermute | solution.py:10
  400.0 1.5 collective-permute-start.3
  401.5 11.7 %collective-permute-done.3 = bf16[4,4,32,1024]{3,2,1,0:T(8,128)(2,1)S(1)} collective-permute-done((bf16[4,4,32,1024]{3,2,1,0:T(8,128)(2,1)S(1)}, bf16[4,4,32,1024]{3,2,1,0:T(8,128)(2,1)S(1)}, u32[]{:S(2)}, u32[]{:S(2)}) %collective-permute-start.3) | collective-permute-done | bytes 1048608 | tf_op jit(solution)/shard_map/ppermute | solution.py:10
  413.3 1.8 fusion.62
  415.1 211.3 %all-gather.6.cloned.1.call-done = bf16[1024,1024]{1,0:T(8,128)(2,1)} async-done(((bf16[8,1024]{1,0:T(8,128)(2,1)}), bf16[1024,1024]{1,0:T(8,128)(2,1)}) %all-gather.6.cloned.1.call-update) | async-done | bytes 2097168 | tf_op jit(solution)/shard_map/all_gather | solution.py:145
  626.3 4.7 convert_reduce_fusion
  631.0 1.3 copy-done.4
  633.1 314.2 %all-gather.8.cloned.1.call-done = bf16[4096,2048]{1,0:T(8,128)(2,1)} async-done(((bf16[32,2048]{1,0:T(8,128)(2,1)}), bf16[4096,2048]{1,0:T(8,128)(2,1)}) %all-gather.8.cloned.1.call-update) | async-done | bytes 16777232 | tf_op jit(solution)/shard_map/all_gather | solution.py:19
  947.3 26.8 %fusion.46 = bf16[1024,1024]{1,0:T(8,128)(2,1)} fusion(bf16[1024,1024]{1,0:T(8,128)(2,1)} %copy-done.4, bf16[4096,2048]{1,0:T(8,128)(2,1)} %all-gather.8.cloned.1.call-done, f32[1024]{0:T(1024)S(1)} %add_rsqrt_fusion.1, f32[1024]{0:T(1024)S(1)} %broadcast_multiply_fusion.1), kind=kOutput, calls=%fused_computation.47 | convolution fusion | flops 17224957952 | bytes 23076864 | tf_op jit(solution)/shard_map/dot_general | solution.py:158
  (64 shorter events, 13.3 us)
Async XLA Ops:
  6.5 11.3 %copy-start = (f32[225,16]{0,1:T(8,128)S(1)}, f32[225,16]{0,1:T(8,128)}, u32[]{:S(2)}) copy-start(f32[225,16]{0,1:T(8,128)} %param.14) | copy-start | bytes 43204
  6.5 7.3 copy-start.2
  6.5 312.3 %all-gather.4.cloned.1.call-start = ((), (), s32[]{:S(2)}) async-start(), calls=%async_computation | async-start | bytes 6340608 | tf_op jit(solution)/shard_map/all_gather | solution.py:128
  7.3 619.1 %all-gather.6.cloned.1.call-start = ((), (), s32[]{:S(2)}) async-start(), calls=%async_computation.1 | async-start | bytes 2113536 | tf_op jit(solution)/shard_map/all_gather | solution.py:145
  8.0 939.3 %all-gather.8.cloned.1.call-start = ((), (), s32[]{:S(2)}) async-start(), calls=%async_computation.2 | async-start | bytes 16908288 | tf_op jit(solution)/shard_map/all_gather | solution.py:19
  13.9 3.1 copy-start.5
  15.6 15.4 %collective-permute-start = (bf16[4,4,32,1024]{3,2,1,0:T(8,128)(2,1)}, bf16[4,4,32,1024]{3,2,1,0:T(8,128)(2,1)S(1)}, u32[]{:S(2)}, u32[]{:S(2)}) collective-permute-start(bf16[4,4,32,1024]{3,2,1,0:T(8,128)(2,1)} %get-tuple-element.142), channel_id=1, source_target_pairs={{0,120},{8,0},{16,8},{24,16},{32,24},{40,32},{48,40},{56,48},{64,5... | collective-permute-start | bytes 3145736 | tf_op jit(solution)/shard_map/ppermute | solution.py:10
  31.1 12.6 %collective-permute-start.1 = (bf16[4,8,4,1024]{3,2,1,0:T(4,128)(2,1)S(1)}, bf16[4,8,4,1024]{3,2,1,0:T(4,128)(2,1)S(1)}, u32[]{:S(2)}, u32[]{:S(2)}) collective-permute-start(bf16[4,8,4,1024]{3,2,1,0:T(4,128)(2,1)S(1)} %pad_maximum_fusion.2), channel_id=1, source_target_pairs={{0,7},{1,0},{2,1},{3,2},{4,3},{5,4},{6,5},{7,6},{8,15},{9,8},{10,9... | collective-permute-start | bytes 786440 | tf_op jit(solution)/shard_map/ppermute | solution.py:10
  388.2 11.4 %collective-permute-start.2 = (bf16[4,8,4,1024]{3,2,1,0:T(4,128)(2,1)S(1)}, bf16[4,8,4,1024]{3,2,1,0:T(4,128)(2,1)S(1)}, u32[]{:S(2)}, u32[]{:S(2)}) collective-permute-start(bf16[4,8,4,1024]{3,2,1,0:T(4,128)(2,1)S(1)} %slice.46), channel_id=1, source_target_pairs={{0,1},{1,2},{2,3},{3,4},{4,5},{5,6},{6,7},{7,0},{8,9},{9,10},{10,1... | collective-permute-start | bytes 786440 | tf_op jit(solution)/shard_map/ppermute | solution.py:10
  399.6 226.7 %copy-start.3 = (bf16[4,8,32,1024]{3,2,1,0:T(8,128)(2,1)S(1)}, bf16[4,8,32,1024]{3,2,1,0:T(8,128)(2,1)}, u32[]{:S(2)}) copy-start(bf16[4,8,32,1024]{3,2,1,0:T(8,128)(2,1)} %param.9) | copy-start | bytes 6291460
  400.0 13.2 %collective-permute-start.3 = (bf16[4,4,32,1024]{3,2,1,0:T(8,128)(2,1)S(1)}, bf16[4,4,32,1024]{3,2,1,0:T(8,128)(2,1)S(1)}, u32[]{:S(2)}, u32[]{:S(2)}) collective-permute-start(bf16[4,4,32,1024]{3,2,1,0:T(8,128)(2,1)S(1)} %fusion.68), channel_id=1, source_target_pairs={{0,8},{8,16},{16,24},{24,32},{32,40},{40,48},{48,56},{56,64},{64,7... | collective-permute-start | bytes 3145736 | tf_op jit(solution)/shard_map/ppermute | solution.py:10
  631.0 1.4 copy-start.4
  947.3 26.8 %copy-start.1 = (f32[225,16]{0,1:T(8,128)S(1)}, f32[225,16]{0,1:T(8,128)}, u32[]{:S(2)}) copy-start(f32[225,16]{0,1:T(8,128)} %param.14) | copy-start | bytes 43204
Sparse Core Ops, SparseCore 0:
  9.0 309.7 all-gather.3
  320.5 305.8 all-gather.5
  628.0 319.1 all-gather.7
where the time goes:
time: 981 us
  waiting for transfers between devices  838 us (85%)
  matrix products  62.2 us (6%)
  local copies, waits for them, and re-layouts  39.9 us (4%)
  between operations  13.3 us (1%)
  starting transfers between devices  11.5 us (1%)
  other arithmetic  10.9 us (1%)
    all_gather x1, waiting for transfers between devices, sent_together(): lax.all_gather(both, axis, axis=dim, tiled=True)  314 us
    all_gather x1, waiting for transfers between devices, per_device(): lax.all_gather(qkv_weight, ('lat', 'lon'), axis=0, tiled=True)  275 us
    all_gather x1, waiting for transfers between devices, per_device(): lax.all_gather(proj_weight, ('lat', 'lon'), axis=0, tiled=True)  211 us
    ppermute x4, waiting for transfers between devices, from_behind(): return lax.ppermute(value, axis, pairs)  36 us
    dot_general x1, matrix products, per_device(): hidden_sum = jnp.dot(hidden, down_part, preferred_element_type=jnp.float32)  26.8 us
  transfers between devices with their start and end apart: 7, of which 7 were waited for; matrix products, arithmetic and copies ran while one was open for 9% of the time, Pallas kernels for 0%

commit v1 on v0

v1 whole, which is shorter than its diff:
```python
import jax
import jax.numpy as jnp
from jax import lax
from jax.experimental import pallas as pl
from jax.experimental.pallas import tpu as pltpu
from jax.sharding import PartitionSpec as P

MESH = pl.DeviceIdType.MESH
BF = jnp.bfloat16
F32 = jnp.float32
D = 1024
BLK = 512
FAR = -1e30

PIECES = {
    "qa": (0, 0, 8, "xyz"),
    "qb": (0, 8, 8, "yzx"),
    "qc": (0, 16, 8, "zxy"),
    "ua": (2, 0, 16, "xyz"),
    "ub": (2, 16, 8, "yzx"),
    "pc": (1, 0, 8, "zxy"),
    "uc": (2, 24, 8, "zxy"),
    "da": (3, 0, 8, "xyz"),
    "db": (3, 8, 16, "yzx"),
    "dc": (3, 24, 8, "zxy"),
}
NAMES = list(PIECES)
PER = 15

FIRST = ["qa", "qb", "qc"]
LATER = ["pc", "ua", "ub", "uc", "da", "db", "dc"]
PLAN = [
    ("start", [(2, n) for n in FIRST] + [(3, n) for n in FIRST] + [(4, n) for n in FIRST]),
    ("start", [(2, n) for n in LATER[:4]] + [(3, n) for n in LATER[:4]]),
    ("norm", [(5, n) for n in FIRST] + [(4, n) for n in LATER[:4]]),
    ("norm", [(6, n) for n in FIRST] + [(7, n) for n in FIRST]),
    ("qkv1", [(2, n) for n in LATER[4:]]),
    ("qkv2", [(3, n) for n in LATER[4:]]),
    ("qkv3", [(5, "ub"), (5, "pc")]),
    ("att0", [(4, "db"), (6, "ub"), (6, "pc")]),
    ("att3", [(5, "ua")]),
    ("att5", [(5, "uc"), (4, "da"), (4, "dc")]),
    ("att10", [(6, "ua")]),
    ("att12", [(6, "uc"), (7, "pc")]),
    ("proj0", [(5, "da"), (5, "db")]),
    ("proj2", [(5, "dc")]),
    ("up0", [(7, "ua"), (7, "ub"), (7, "uc")]),
    ("up2", [(6, "da")]),
    ("up4", [(6, "dc")]),
    ("up5", [(6, "db")]),
    ("down0", [(7, "da"), (7, "db"), (7, "dc")]),
]


def planned(slot):
    steps = []
    for name, listed in PLAN:
        if name == slot:
            steps += listed
    return steps


def block_kernel(
    tok, wq_in, wp_in, wu_in, wd_in, bias, keys,
    out,
    wq, wp, wu, wd, ext, normed, qkv, att, hid, back, side,
    w_send, w_recv, own_sem, h_send, h_recv, r_send, r_recv, t_sem,
):
    lat = lax.axis_index("lat")
    lon = lax.axis_index("lon")
    core = lat % 2
    y = (lat // 2) % 4
    z_lo = lat // 8
    x = lon % 4
    z_hi = lon // 4
    at = {"x": x, "y": y, "z": z_hi * 2 + z_lo}

    def device(over, partner=False):
        c = dict(at)
        c.update(over)
        k = 1 - core if partner else core
        return {"lat": ((c["z"] % 2) * 4 + c["y"]) * 2 + k, "lon": (c["z"] // 2) * 4 + c["x"]}

    def near(axis, by):
        return (at[axis] + by + 4) % 4

    def shifted(d_lat, d_lon):
        return {"lat": (lat + d_lat + 16) % 16, "lon": (lon + d_lon + 8) % 8}

    held = (wq, wp, wu, wd)
    shards = (wq_in, wp_in, wu_in, wd_in)

    def region(name, c, where):
        which, first, rows, _ = PIECES[name]
        ref = held[which]

        def part(axis):
            v = where[axis]
            if v is None:
                return slice(None)
            if isinstance(v, tuple):
                return pl.ds(2 * v[1], 2)
            return v

        v = where["z"]
        if v is None:
            lo, hi = slice(None), slice(None)
        elif isinstance(v, tuple):
            lo, hi = v[1], slice(None)
        else:
            lo, hi = v % 2, v // 2
        return ref.at[lo, part("y"), c, hi, part("x"), pl.ds(first, rows)]

    def weight_copy(name, slot, where, to, partner=False, src=None):
        k = NAMES.index(name) * PER + slot
        there = region(name, core, where)
        return pltpu.make_async_remote_copy(
            src_ref=there if src is None else src,
            dst_ref=there,
            send_sem=w_send.at[k],
            recv_sem=w_recv.at[k],
            device_id=device(to, partner),
            device_id_type=MESH,
        )

    def copies(name):
        a1, a2, a3 = PIECES[name][3]
        made = {}
        here = dict(at)

        def add(slot, sent, came, to, partner=False):
            made[slot] = (
                lambda: weight_copy(name, slot, sent, to, partner),
                lambda: weight_copy(name, slot, came, to, partner),
            )

        for slot, by in ((0, 1), (1, 3), (2, 2)):
            add(slot, here, {**here, a1: near(a1, -by)}, {a1: near(a1, by)})
        base = 3
        for axis, full, half in ((a2, [a1], a1), (a3, [a1, a2], a1)):
            whole = {**here, **{f: None for f in full}}
            add(base, whole, {**whole, axis: near(axis, -1)}, {axis: near(axis, 1)})
            add(base + 1, whole, {**whole, axis: near(axis, 1)}, {axis: near(axis, -1)})
            first = {**whole, half: ("h", 0)}
            second = {**whole, half: ("h", 1)}
            far = near(axis, 2)
            add(base + 2, {**first, axis: near(axis, -1)}, {**first, axis: far}, {axis: near(axis, 1)})
            add(base + 3, {**second, axis: near(axis, 1)}, {**second, axis: far}, {axis: near(axis, -1)})
            base += 4
        plane = {**here, a1: None, a2: None}
        for slot, by in ((11, 0), (12, 1), (13, 3), (14, 2)):
            sent = {**plane, a3: near(a3, by)}
            add(slot, sent, sent, {}, True)
        return made

    def send(name, *slots):
        for s in slots:
            copies(name)[s][0]().start()

    def came(name, *slots):
        for s in slots:
            copies(name)[s][1]().wait_recv()

    def step(number, name):
        if number == 1:
            send(name, 0, 1, 2)
        elif number == 2:
            came(name, 0, 1, 2)
            send(name, 3, 4)
        elif number == 3:
            came(name, 3, 4)
            send(name, 5, 6)
        elif number == 4:
            came(name, 5, 6)
            send(name, 7, 8, 11)
        elif number == 5:
            came(name, 7, 8)
            send(name, 9, 10, 12, 13)
        elif number == 6:
            came(name, 9, 10)
            send(name, 14)
        else:
            came(name, 11, 12, 13, 14)

    def pump(slot):
        for number, name in planned(slot):
            step(number, name)

    def pump_at(prefix, i, count):
        for k in range(count):
            if planned(f"{prefix}{k}"):
                @pl.when(i == k)
                def _(k=k):
                    pump(f"{prefix}{k}")

    def geometry(b):
        ahead = b < 2
        right = b % 2 == 0
        mine = pl.ds(4, 4) if ahead else pl.ds(0, 4)
        other = pl.ds(0, 4) if ahead else pl.ds(4, 4)
        d_lat = 1 if ahead else -1
        d_lon = 1 if right else -1
        off = 0 if right else 1
        edge = 4 if right else 0
        border = 0 if right else 3
        return mine, other, d_lat, d_lon, off, edge, border

    def halo(b):
        mine, other, d_lat, d_lon, off, edge, border = geometry(b)
        listed = (
            (tok.at[b, other], ext.at[b, other, pl.ds(off, 4)], (-d_lat, 0)),
            (tok.at[b, mine, border], ext.at[b, mine, edge], (0, -d_lon)),
            (tok.at[b, other, border], ext.at[b, other, edge], (-d_lat, -d_lon)),
        )
        return [
            pltpu.make_async_remote_copy(
                src_ref=s, dst_ref=d, send_sem=h_send.at[3 * b + k], recv_sem=h_recv.at[3 * b + k],
                device_id=shifted(*to), device_id_type=MESH,
            )
            for k, (s, d, to) in enumerate(listed)
        ]

    def local_tokens(b):
        mine, _, _, _, off, _, _ = geometry(b)
        return pltpu.make_async_copy(tok.at[b, mine], ext.at[b, mine, pl.ds(off, 4)], t_sem.at[b])

    def returns(b):
        mine, other, d_lat, d_lon, off, edge, _ = geometry(b)
        listed = (
            (back.at[b, other, pl.ds(off, 4)], out.at[b, other], (d_lat, 0)),
            (back.at[b, mine, edge], side.at[b, mine], (0, d_lon)),
            (back.at[b, other, edge], side.at[b, other], (d_lat, d_lon)),
        )
        return [
            pltpu.make_async_remote_copy(
                src_ref=s, dst_ref=d, send_sem=r_send.at[3 * b + k], recv_sem=r_recv.at[3 * b + k],
                device_id=shifted(*to), device_id_type=MESH,
            )
            for k, (s, d, to) in enumerate(listed)
        ]

    def own(which):
        return pltpu.make_async_copy(
            shards[which], held[which].at[z_lo, y, core, z_hi, x], own_sem.at[which]
        )

    for which in range(4):
        own(which).start()
    for b in range(4):
        local_tokens(b).start()

    barrier = pltpu.get_barrier_semaphore()
    peers = [device({a: near(a, by)}) for a in "xyz" for by in (1, 2, 3)]
    peers.append(device({}, True))
    peers += [shifted(i, j) for i in (-1, 0, 1) for j in (-1, 0, 1) if (i, j) != (0, 0)]
    for peer in peers:
        pl.semaphore_signal(barrier, inc=1, device_id=peer, device_id_type=MESH)
    pl.semaphore_wait(barrier, len(peers))

    for which in range(4):
        own(which).wait()
    for n in FIRST:
        step(1, n)
    for b in range(4):
        for c in halo(b):
            c.start()
    for n in LATER:
        step(1, n)

    pump("start")

    early = lax.broadcasted_iota(jnp.int32, (64, D), 0) % 8 < 4

    def window_tokens(b, w):
        left = ext[b, :, w].astype(F32).reshape(64, D)
        right = ext[b, :, w + 1].astype(F32).reshape(64, D)
        return jnp.where(early, right, left)

    def layer_norm(v):
        centre = jnp.mean(v, axis=-1, keepdims=True)
        moved = v - centre
        spread = jnp.mean(moved * moved, axis=-1, keepdims=True)
        return (moved * lax.rsqrt(spread + 1e-05)).astype(BF)

    for b in range(4):
        local_tokens(b).wait()
        for c in halo(b):
            c.wait_recv()

    def norm_one(i, _):
        rows = pl.ds(pl.multiple_of(i * 64, 64), 64)
        normed[rows] = layer_norm(window_tokens(i // 4, i % 4))
        return 0

    lax.fori_loop(0, 16, norm_one, 0)
    pump("norm")

    def qkv_one(i, _):
        pump_at("qkv", i, 4)
        w = wq[i // 2, pl.ds((i % 2) * 2, 2)].reshape(768, D)
        got = lax.dot_general(normed[...], w, (((1,), (1,)), ((), ())), preferred_element_type=F32)
        qkv[:, pl.ds(pl.multiple_of(i * 768, 768), 768)] = got.astype(BF)
        return 0

    lax.fori_loop(0, 4, qkv_one, 0)

    lane_head = lax.broadcasted_iota(jnp.int32, (64, 256), 1) // 64
    pick = [lane_head == h for h in range(4)]
    ones_at = (
        lax.broadcasted_iota(jnp.int32, (256, 256), 0) // 64
        == lax.broadcasted_iota(jnp.int32, (256, 256), 1) // 64
    )
    ones = jnp.where(ones_at, 1.0, 0.0).astype(BF)
    first_half = lax.broadcasted_iota(jnp.int32, (64, 128), 1) < 64
    q_cell = lax.broadcasted_iota(jnp.int32, (64, 128), 0)
    k_cell = lax.broadcasted_iota(jnp.int32, (64, 128), 1) % 64
    itself = q_cell == k_cell
    parted = (q_cell < 32) != (k_cell < 32)

    def spread_heads(v):
        wide = v.astype(F32)
        return jnp.concatenate([jnp.where(p, wide, 0.0).astype(BF) for p in pick], axis=0)

    def attend_one(i, _):
        pump_at("att", i, 16)
        rows = pl.ds(pl.multiple_of(i * 64, 64), 64)
        at_end = jnp.where(i < 8, lat, (lat + 15) % 16) == 15
        end_value = jnp.where(at_end, FAR, 0.0)
        mask = jnp.where(itself, 0.0, jnp.broadcast_to(keys[pl.ds(i, 1)], (64, 128)))
        mask = jnp.where(parted, mask + end_value, mask)
        for g in range(4):
            q = qkv[rows, pl.ds(256 * g, 256)]
            k = qkv[rows, pl.ds(D + 256 * g, 256)]
            v = qkv[rows, pl.ds(2 * D + 256 * g, 256)]
            scores = lax.dot_general(
                q, spread_heads(k), (((1,), (1,)), ((), ())), preferred_element_type=F32
            )
            weights = []
            for t in range(2):
                s = scores[:, 128 * t : 128 * t + 128] * 0.125 + bias[g, :, pl.ds(128 * t, 128)] + mask
                top_a = jnp.max(jnp.where(first_half, s, -jnp.inf), axis=1, keepdims=True)
                top_b = jnp.max(jnp.where(first_half, -jnp.inf, s), axis=1, keepdims=True)
                weights.append(jnp.exp(s - jnp.where(first_half, top_a, top_b)).astype(BF))
            e = jnp.concatenate(weights, axis=1)
            total = jnp.dot(e, ones, preferred_element_type=F32)
            context = jnp.dot(e, spread_heads(v), preferred_element_type=F32) / total
            att[rows, pl.ds(256 * g, 256)] = context.astype(BF)
        return 0

    lax.fori_loop(0, 16, attend_one, 0)

    def proj_one(b, _):
        pump_at("proj", b, 4)
        rows = pl.ds(pl.multiple_of(b * 256, 256), 256)
        got = lax.dot_general(
            att[rows], wp[...].reshape(D, D), (((1,), (1,)), ((), ())), preferred_element_type=F32
        )
        for w in range(4):
            part = pl.ds(pl.multiple_of(b * 256 + w * 64, 64), 64)
            whole = (window_tokens(b, w) + got[64 * w : 64 * w + 64]).astype(BF)
            att[part] = whole
            normed[part] = layer_norm(whole.astype(F32))
        return 0

    lax.fori_loop(0, 4, proj_one, 0)

    def up_one(i, _):
        pump_at("up", i, 8)
        w = wu[i // 4, i % 4].reshape(BLK, D)
        got = lax.dot_general(normed[...], w, (((1,), (1,)), ((), ())), preferred_element_type=F32)
        hid[:, pl.ds(pl.multiple_of(i * BLK, BLK), BLK)] = jax.nn.gelu(got).astype(BF)
        return 0

    lax.fori_loop(0, 8, up_one, 0)
    pump("down0")

    def down_one(b):
        mine, other, _, _, off, edge, _ = geometry(b)
        rows = pl.ds(b * 256, 256)
        got = jnp.dot(hid[rows], wd[...].reshape(4 * D, D), preferred_element_type=F32)
        got = got + att[rows].astype(F32)
        for j in range(5):
            left = got[64 * max(j - 1, 0) : 64 * max(j - 1, 0) + 64]
            right = got[64 * min(j, 3) : 64 * min(j, 3) + 64]
            whole = jnp.where(early, left, right).astype(BF).reshape(8, 8, D)
            back[b, :, j] = whole
            if j != edge:
                out[b, mine, j - off] = whole[4:] if b < 2 else whole[:4]
        for c in returns(b):
            c.start()

    for b in (0, 2, 1, 3):
        down_one(b)

    early_cols = lax.broadcasted_iota(jnp.int32, (64, D), 0) % 8 < 4
    for b in (0, 2, 1, 3):
        border = geometry(b)[6]
        for c in returns(b):
            c.wait_recv()
        here = out[b, :, border].astype(F32).reshape(64, D)
        came_in = side[b].astype(F32).reshape(64, D)
        both = jnp.where(early_cols, came_in, here) if b % 2 == 0 else jnp.where(early_cols, here, came_in)
        out[b, :, border] = both.astype(BF).reshape(8, 8, D)

    for n in NAMES:
        for s in range(PER):
            copies(n)[s][0]().wait_send()
    for b in range(4):
        for c in halo(b) + returns(b):
            c.wait_send()


def window_order(values):
    return jnp.roll(values, (4, 4), axis=(-2, -1)).reshape(values.shape[:-2] + (64,))


def per_device(tokens, qkv_weight, proj_weight, up_weight, down_weight, bias_table, sea_mask):
    head_count = bias_table.shape[1]
    lat = lax.axis_index("lat")
    lon = lax.axis_index("lon")

    cells = window_order(jnp.arange(64, dtype=jnp.int32).reshape(8, 8))
    row_of, col_of = cells // 8, cells % 8
    offsets = (row_of[:, None] - row_of[None, :] + 7) * 15 + (col_of[:, None] - col_of[None, :] + 7)
    one_hot = (offsets.reshape(-1)[:, None] == jnp.arange(bias_table.shape[0], dtype=jnp.int32)).astype(F32)
    bias = jnp.dot(one_hot, bias_table, precision=lax.Precision.HIGHEST)
    bias = bias.reshape(64, 64, head_count // 4, 4).transpose(2, 0, 3, 1).reshape(head_count // 4, 64, 256)

    around = jnp.pad(sea_mask, ((8, 16), (8, 16)), mode="wrap")
    rows = []
    for b in range(4):
        r0 = 8 * (lat if b < 2 else lat - 1) + 8 + 4
        c0 = 32 * lon - (0 if b % 2 == 0 else 8) + 8 + 4
        cut = lax.dynamic_slice(around, (r0, c0), (8, 32))
        rows.append(window_order(cut.reshape(8, 4, 8).transpose(1, 0, 2)))
    keys = jnp.where(jnp.concatenate(rows, axis=0) == 1, 0.0, FAR).astype(F32)
    keys = jnp.concatenate([keys, keys], axis=1)

    hbm = pl.BlockSpec(memory_space=pl.ANY)
    vmem = pl.BlockSpec(memory_space=pltpu.VMEM)
    shard = (2, 4, 2, 2, 4)
    tile = (4, 8, 4, 8, D)
    messages = len(NAMES) * PER
    dma = pltpu.SemaphoreType.DMA
    out = pl.pallas_call(
        block_kernel,
        out_shape=jax.ShapeDtypeStruct(tile, BF),
        in_specs=[hbm] * 5 + [vmem, vmem],
        out_specs=vmem,
        scratch_shapes=[
            pltpu.VMEM(shard + (24, D), BF),
            pltpu.VMEM(shard + (8, D), BF),
            pltpu.VMEM(shard + (32, D), BF),
            pltpu.VMEM(shard + (32, D), BF),
            pltpu.VMEM((4, 8, 5, 8, D), BF),
            pltpu.VMEM((1024, D), BF),
            pltpu.VMEM((1024, 3 * D), BF),
            pltpu.VMEM((1024, D), BF),
            pltpu.VMEM((1024, 4 * D), BF),
            pltpu.VMEM((4, 8, 5, 8, D), BF),
            pltpu.VMEM((4, 8, 8, D), BF),
            dma((messages,)),
            dma((messages,)),
            dma((4,)),
            dma((12,)),
            dma((12,)),
            dma((12,)),
            dma((12,)),
            dma((4,)),
        ],
        compiler_params=pltpu.CompilerParams(
            collective_id=0, has_side_effects=True, vmem_limit_bytes=67043328
        ),
        name="swin_block",
    )(tokens.reshape(tile), qkv_weight, proj_weight, up_weight, down_weight, bias, keys)
    return out.reshape(tokens.shape)


def solution(mesh):
    placed = (
        P(None, "lat", "lon", None),
        P(("lat", "lon"), None),
        P(("lat", "lon"), None),
        P(("lat", "lon"), None),
        P(("lat", "lon"), None),
        P(),
        P(),
    )
    return jax.shard_map(
        per_device,
        mesh=mesh,
        in_specs=placed,
        out_specs=P(None, "lat", "lon", None),
        check_vma=False,
    )
```

time: 981 us -> 136 us (0.14)
  waiting for transfers between devices: 838 us -> 0 us
  Pallas kernels: 0 us -> 122 us
  matrix products: 62.2 us -> 2.56 us
  local copies, waits for them, and re-layouts: 39.9 us -> 7.34 us
  between operations: 13.3 us -> 0.1 us
  starting transfers between devices: 11.5 us -> 0 us
    all_gather x3 -> x0, waiting for transfers between devices: 800 us -> none  [the longest x1 314 us: sent_together(): lax.all_gather(both, axis, axis=dim, tiled=True)]
    pallas_call x0 -> x1, Pallas kernels: none -> 122 us  [per_device(): pl.pallas_call(block_kernel, out_shape=jax.ShapeDtypeStruct(tile, BF), in...]
    dot_general x8 -> x1, matrix products: 51.8 us -> 2.56 us  [per_device(): bias = jnp.dot(one_hot, bias_table, precision=lax.Precision.HIGHEST)]
    ppermute x4 -> x0, waiting for transfers between devices: 36 us -> none  [from_behind(): return lax.ppermute(value, axis, pairs)]
    dynamic_slice x16 -> x1, local copies, waits for them, and re-layouts: 13.9 us -> 0.11 us  [per_device(): cut = lax.dynamic_slice(around, (r0, c0), (8, 32))]
    ppermute x4 -> x0, starting transfers between devices: 11.4 us -> none  [from_behind(): return lax.ppermute(value, axis, pairs)]
    reshape x14 -> x12, local copies, waits for them, and re-layouts: 12.9 us -> 2.34 us  [the longest x3 1.62 us: per_device(): bias.reshape(64, 64, head_count // 4, 4).transpose(2, 0, 3, 1)]
    sub x4 -> x0, matrix products: 10.4 us -> none  [one_group(): weights = jnp.exp(scores - row_top)]
  transfers between devices with their start and end apart: 7 -> 0, of which waited for: 7 -> 0; matrix products, arithmetic and copies ran while one was open for 9% -> 0% of each run, Pallas kernels for 0% -> 0%
where the time goes in v1:
time: 136 us; the launch traced here: 135 us
  Pallas kernels  122 us (90%)
  local copies, waits for them, and re-layouts  7.34 us (5%)
  other arithmetic  3.49 us (3%)
  matrix products  2.56 us (2%)
    pallas_call x1, Pallas kernels, per_device(): pl.pallas_call(block_kernel, out_shape=jax.ShapeDtypeStruct(tile, BF), in...  122 us
    unnamed x3, local copies, waits for them, and re-layouts  3.19 us

profile of v1, /device:TPU:1, one launch (start us, length us, event | category | flops | bytes accessed | tf_op | source)
XLA Modules:
  0.0 135.2 jit_solution(14477431299066481785)
XLA Ops:
  0.0 0.0 copy-start
  0.0 0.1 fusion.8
  0.1 0.1 pad_add_fusion.11
  0.2 0.1 reshape.191
  0.3 0.7 slice.88
  1.0 0.7 slice.89
  1.7 0.1 add_add_fusion
  1.8 0.1 add.114
  1.9 0.9 pad_add_fusion.1
  2.8 0.1 slice.108
  2.9 1.1 pad_add_fusion
  3.9 0.1 fusion.3
  4.1 0.1 reshape.194
  4.1 0.1 reshape.200
  4.2 0.1 reshape.198
  4.3 0.1 reshape.196
  4.4 0.1 slice_add_fusion.2
  4.5 0.1 pad_add_fusion.7
  4.6 0.1 reshape.197
  4.6 0.1 slice_add_fusion.1
  4.7 0.1 pad_add_fusion.8
  4.8 0.1 reshape.199
  4.9 0.1 slice_add_fusion
  5.0 0.1 pad_add_fusion.9
  5.1 0.1 reshape.201
  5.1 0.1 slice_add_fusion.3
  5.2 0.1 pad_add_fusion.6
  5.3 0.1 reshape.195
  5.4 0.7 pad_maximum_fusion.keys
  6.1 0.0 copy-done
  6.1 2.6 %fusion = f32[4096,16]{0,1:T(8,128)S(1)} fusion(f32[225,16]{0,1:T(8,128)S(1)} %copy-done, s32[4096]{0:T(1024)S(1)} %add.114), kind=kOutput, calls=%fused_computation.1 | convolution fusion | flops 177868800 | bytes 292928 | tf_op jit(solution)/shard_map/dot_general | solution.py:426
  8.7 0.2 reshape.192
  8.9 0.3 copy.15
  9.2 1.0 reshape.193.bias
  10.3 121.7 %swin_block.1 = bf16[4,8,4,8,1024]{4,3,2,1,0:T(8,128)(2,1)} custom-call(bf16[4,8,4,8,1024]{4,3,2,1,0:T(8,128)(2,1)} %bitcast.13, bf16[24,1024]{1,0:T(8,128)(2,1)} %wq_in.1, bf16[8,1024]{1,0:T(8,128)(2,1)} %wp_in.1, bf16[32,1024]{1,0:T(8,128)(2,1)} %wu_in.1, bf16[32,1024]{1,0:T(8,128)(2,1)} %wd_in.1, f32[4,64,256]{2,1,0:T(8,128)} %reshape.193.bias, ...), custom_call_target="tpu_custom_call" | custom-call | tf_op jit(solution)/shard_map/swin_block/pallas_call | solution.py:445
  132.0 3.2 %copy.17 = bf16[4,8,32,1024]{3,2,1,0:T(8,128)(2,1)} copy(bf16[4,8,32,1024]{3,2,1,0:T(8,128)(2,1)} %bitcast.12) | data formatting | bytes 4194304
  (14 shorter events, 0.1 us)
Async XLA Ops:
  0.0 6.1 %copy-start = (f32[225,16]{0,1:T(8,128)S(1)}, f32[225,16]{0,1:T(8,128)}, u32[]{:S(2)}) copy-start(f32[225,16]{0,1:T(8,128)} %param.12) | copy-start | bytes 43204

commit v2 on v1

--- a/solution.py
+++ b/solution.py
@@ -27,43 +27,90 @@
 NAMES = list(PIECES)
 PER = 15
 
-FIRST = ["qa", "qb", "qc"]
-LATER = ["pc", "ua", "ub", "uc", "da", "db", "dc"]
 PLAN = [
-    ("start", [(2, n) for n in FIRST] + [(3, n) for n in FIRST] + [(4, n) for n in FIRST]),
-    ("start", [(2, n) for n in LATER[:4]] + [(3, n) for n in LATER[:4]]),
-    ("norm", [(5, n) for n in FIRST] + [(4, n) for n in LATER[:4]]),
-    ("norm", [(6, n) for n in FIRST] + [(7, n) for n in FIRST]),
-    ("qkv1", [(2, n) for n in LATER[4:]]),
-    ("qkv2", [(3, n) for n in LATER[4:]]),
-    ("qkv3", [(5, "ub"), (5, "pc")]),
-    ("att0", [(4, "db"), (6, "ub"), (6, "pc")]),
-    ("att3", [(5, "ua")]),
-    ("att5", [(5, "uc"), (4, "da"), (4, "dc")]),
-    ("att10", [(6, "ua")]),
-    ("att12", [(6, "uc"), (7, "pc")]),
-    ("proj0", [(5, "da"), (5, "db")]),
-    ("proj2", [(5, "dc")]),
-    ("up0", [(7, "ua"), (7, "ub"), (7, "uc")]),
-    ("up2", [(6, "da")]),
-    ("up4", [(6, "dc")]),
-    ("up5", [(6, "db")]),
-    ("down0", [(7, "da"), (7, "db"), (7, "dc")]),
+    ("start", 1, "qa"),
+    ("start", 1, "qb"),
+    ("start", 1, "qc"),
+    ("start", 1, "pc"),
+    ("start", 1, "ua"),
+    ("start", 1, "ub"),
+    ("start", 1, "uc"),
+    ("start", 1, "da"),
+    ("start", 1, "db"),
+    ("start", 1, "dc"),
+    ("normA", 2, "qa"),
+    ("normA", 2, "qb"),
+    ("normA", 2, "qc"),
+    ("normA", "halo", "columns"),
+    ("normA", "halo", "rows"),
+    ("normA", 3, "qc"),
+    ("normA", 3, "qa"),
+    ("normA", 3, "qb"),
+    ("normA", 2, "ub"),
+    ("normA", 2, "pc"),
+    ("normA", 2, "ua"),
+    ("normA", 2, "uc"),
+    ("normA", 2, "da"),
+    ("normA", 2, "db"),
+    ("normA", 2, "dc"),
+    ("normA", 4, "qb"),
+    ("normB", 3, "ub"),
+    ("normB", 4, "qc"),
+    ("normB", 3, "db"),
+    ("normB", 3, "pc"),
+    ("normB", 4, "qa"),
+    ("qkv0", 3, "uc"),
+    ("qkv0", 3, "dc"),
+    ("qkv0", 3, "ua"),
+    ("qkv0", 3, "da"),
+    ("qkv0", 5, "qa"),
+    ("qkv0", 5, "qb"),
+    ("qkv0", 5, "qc"),
+    ("qkv0", 4, "ub"),
+    ("qkv0", 4, "pc"),
+    ("qkv0", 4, "ua"),
+    ("qkv0", 6, "qa"),
+    ("qkv0", 6, "qb"),
+    ("qkv0", 7, "qa"),
+    ("qkv0", 6, "qc"),
+    ("qkv0", 7, "qb"),
+    ("qkv0", 7, "qc"),
+    ("qkv2", 5, "ub"),
+    ("qkv2", 4, "db"),
+    ("qkv3", 5, "pc"),
+    ("qkv3", 4, "uc"),
+    ("att2", 5, "ua"),
+    ("att2", 6, "ub"),
+    ("att2", 4, "da"),
+    ("att5", 6, "pc"),
+    ("att8", 7, "ub"),
+    ("att9", 7, "pc"),
+    ("att13", 5, "uc"),
+    ("att13", 4, "dc"),
+    ("att14", 6, "ua"),
+    ("proj2", 7, "ua"),
+    ("proj2", 5, "db"),
+    ("proj3", 6, "uc"),
+    ("up0", 5, "da"),
+    ("up0", 7, "uc"),
+    ("up2", 5, "dc"),
+    ("up3", 6, "da"),
+    ("up3", 6, "db"),
+    ("up5", 7, "da"),
+    ("up5", 7, "db"),
+    ("up5", 6, "dc"),
+    ("up7", 7, "dc"),
 ]
 
 
 def planned(slot):
-    steps = []
-    for name, listed in PLAN:
-        if name == slot:
-            steps += listed
-    return steps
+    return [(what, name) for where, what, name in PLAN if where == slot]
 
 
 def block_kernel(
-    tok, wq_in, wp_in, wu_in, wd_in, bias, keys,
+    tok, wq_in, wp_in, wu_in, wd_in, table, sea,
     out,
-    wq, wp, wu, wd, ext, normed, qkv, att, hid, back, side,
+    wq, wp, wu, wd, ext, normed, qkv, att, hid, back, side, spread, bias, keys,
     w_send, w_recv, own_sem, h_send, h_recv, r_send, r_recv, t_sem,
 ):
     lat = lax.axis_index("lat")
@@ -183,8 +230,13 @@
             came(name, 11, 12, 13, 14)
 
     def pump(slot):
-        for number, name in planned(slot):
-            step(number, name)
+        for what, name in planned(slot):
+            if what == "halo":
+                for b in range(4):
+                    for k in (1,) if name == "columns" else (0, 2):
+                        halo(b)[k].start()
+            else:
+                step(what, name)
 
     def pump_at(prefix, i, count):
         for k in range(count):
@@ -259,41 +311,89 @@
 
     for which in range(4):
         own(which).wait()
-    for n in FIRST:
-        step(1, n)
+    pump("start")
+
+    pump("keys")
+    spot = lax.broadcasted_iota(jnp.int32, (256, 512), 1)
+    spot_col = spot % 8
+    spot_window = spot // 128
+    grid_col = lax.broadcasted_iota(jnp.int32, (256, 512), 0)
+    own_row = lax.broadcasted_iota(jnp.int32, (8, 512), 0) == (lax.broadcasted_iota(jnp.int32, (8, 512), 1) // 8) % 8
     for b in range(4):
-        for c in halo(b):
-            c.start()
-    for n in LATER:
-        step(1, n)
-
-    pump("start")
-
-    early = lax.broadcasted_iota(jnp.int32, (64, D), 0) % 8 < 4
-
-    def window_tokens(b, w):
-        left = ext[b, :, w].astype(F32).reshape(64, D)
-        right = ext[b, :, w + 1].astype(F32).reshape(64, D)
+        row = lat if b < 2 else (lat + 15) % 16
+        block = lon * 4 + (0 if b % 2 == 0 else 31)
+        upper = sea[pl.ds(pl.multiple_of(row * 8, 8), 8)]
+        lower = sea[pl.ds(pl.multiple_of(((row + 1) % 16) * 8, 8), 8)]
+        band = jnp.concatenate([upper[4:], lower[:4]], axis=0)
+        open_at = jnp.where(band == 1, 1.0, 0.0).astype(BF)
+        wanted = ((block + spot_window + jnp.where(spot_col < 4, 1, 0)) * 8 + spot_col) % 256
+        chosen = jnp.where(grid_col == wanted, 1.0, 0.0).astype(BF)
+        found = jnp.dot(open_at, chosen, preferred_element_type=F32)
+        found = jnp.sum(jnp.where(own_row, found, 0.0), axis=0, keepdims=True)
+        closed = jnp.where(found > 0.5, 0.0, FAR)
+        for w in range(4):
+            keys[4 * b + w : 4 * b + w + 1] = closed[:, 128 * w : 128 * w + 128]
+
+    pump("bias")
+    lane = lax.broadcasted_iota(jnp.int32, (16, 256), 1)
+    head_row = lax.broadcasted_iota(jnp.int32, (16, 256), 0)
+    lane_row = (lane % 64) // 8
+    col_step = (lax.broadcasted_iota(jnp.int32, (8, 256), 0) + 4) % 8 - (
+        lax.broadcasted_iota(jnp.int32, (8, 256), 1) + 4
+    ) % 8 + 7
+    for g in range(4):
+        over_lanes = jnp.where(head_row == 4 * g + lane // 64, 1.0, 0.0)
+        wide = jnp.dot(
+            table[...], over_lanes, precision=lax.Precision.HIGHEST, preferred_element_type=F32
+        )
+        for d in range(15):
+            spread[g, d, 0:15] = wide[15 * d : 15 * d + 15]
+
+    def bias_one(i, _):
+        g, r = i // 8, i % 8
+        steps = jnp.zeros((16, 256), F32)
+        for k in range(8):
+            steps = jnp.where(lane_row == k, spread[g, r - k + 7], steps)
+        line = jnp.zeros((8, 256), F32)
+        for d in range(15):
+            line = jnp.where(col_step == d, steps[d : d + 1], line)
+        bias[g, pl.ds(pl.multiple_of(r * 8, 8), 8)] = line
+        return 0
+
+    lax.fori_loop(0, 32, bias_one, 0)
+
+    early = lax.broadcasted_iota(jnp.int32, (32, D), 0) % 8 < 4
+
+    def window_half(b, w, half):
+        rows = pl.ds(jnp.where((b < 2) == (half == 0), 4, 0), 4)
+        left = ext[b, rows, w].astype(F32).reshape(32, D)
+        right = ext[b, rows, w + 1].astype(F32).reshape(32, D)
         return jnp.where(early, right, left)
 
     def layer_norm(v):
         centre = jnp.mean(v, axis=-1, keepdims=True)
         moved = v - centre
-        spread = jnp.mean(moved * moved, axis=-1, keepdims=True)
-        return (moved * lax.rsqrt(spread + 1e-05)).astype(BF)
-
+        spread_of = jnp.mean(moved * moved, axis=-1, keepdims=True)
+        return (moved * lax.rsqrt(spread_of + 1e-05)).astype(BF)
+
+    def norm_half(half):
+        def norm_one(i, _):
+            rows = pl.ds(pl.multiple_of(half * 512 + i * 32, 32), 32)
+            normed[rows] = layer_norm(window_half(i // 4, i % 4, half))
+            return 0
+
+        lax.fori_loop(0, 16, norm_one, 0)
+
+    pump("normA")
     for b in range(4):
         local_tokens(b).wait()
-        for c in halo(b):
-            c.wait_recv()
-
-    def norm_one(i, _):
-        rows = pl.ds(pl.multiple_of(i * 64, 64), 64)
-        normed[rows] = layer_norm(window_tokens(i // 4, i % 4))
-        return 0
-
-    lax.fori_loop(0, 16, norm_one, 0)
-    pump("norm")
+        halo(b)[1].wait_recv()
+    norm_half(0)
+    pump("normB")
+    for b in range(4):
+        halo(b)[0].wait_recv()
+        halo(b)[2].wait_recv()
+    norm_half(1)
 
     def qkv_one(i, _):
         pump_at("qkv", i, 4)
@@ -323,15 +423,19 @@
 
     def attend_one(i, _):
         pump_at("att", i, 16)
-        rows = pl.ds(pl.multiple_of(i * 64, 64), 64)
+        flip = jnp.where(i < 8, 0, 512)
+        top = pl.ds(pl.multiple_of(flip + i * 32, 32), 32)
+        low = pl.ds(pl.multiple_of(512 - flip + i * 32, 32), 32)
+
+        def cut(first):
+            return jnp.concatenate([qkv[top, pl.ds(first, 256)], qkv[low, pl.ds(first, 256)]], axis=0)
+
         at_end = jnp.where(i < 8, lat, (lat + 15) % 16) == 15
         end_value = jnp.where(at_end, FAR, 0.0)
         mask = jnp.where(itself, 0.0, jnp.broadcast_to(keys[pl.ds(i, 1)], (64, 128)))
         mask = jnp.where(parted, mask + end_value, mask)
         for g in range(4):
-            q = qkv[rows, pl.ds(256 * g, 256)]
-            k = qkv[rows, pl.ds(D + 256 * g, 256)]
-            v = qkv[rows, pl.ds(2 * D + 256 * g, 256)]
+            q, k, v = cut(256 * g), cut(D + 256 * g), cut(2 * D + 256 * g)
             scores = lax.dot_general(
                 q, spread_heads(k), (((1,), (1,)), ((), ())), preferred_element_type=F32
             )
@@ -344,20 +448,22 @@
             e = jnp.concatenate(weights, axis=1)
             total = jnp.dot(e, ones, preferred_element_type=F32)
             context = jnp.dot(e, spread_heads(v), preferred_element_type=F32) / total
-            att[rows, pl.ds(256 * g, 256)] = context.astype(BF)
+            att[top, pl.ds(256 * g, 256)] = context[:32].astype(BF)
+            att[low, pl.ds(256 * g, 256)] = context[32:].astype(BF)
         return 0
 
     lax.fori_loop(0, 16, attend_one, 0)
 
-    def proj_one(b, _):
-        pump_at("proj", b, 4)
-        rows = pl.ds(pl.multiple_of(b * 256, 256), 256)
+    def proj_one(i, _):
+        pump_at("proj", i, 4)
+        rows = pl.ds(pl.multiple_of(i * 256, 256), 256)
         got = lax.dot_general(
             att[rows], wp[...].reshape(D, D), (((1,), (1,)), ((), ())), preferred_element_type=F32
         )
-        for w in range(4):
-            part = pl.ds(pl.multiple_of(b * 256 + w * 64, 64), 64)
-            whole = (window_tokens(b, w) + got[64 * w : 64 * w + 64]).astype(BF)
+        for w in range(8):
+            part = pl.ds(pl.multiple_of(i * 256 + w * 32, 32), 32)
+            before = window_half((i % 2) * 2 + w // 4, w % 4, i // 2)
+            whole = (before + got[32 * w : 32 * w + 32]).astype(BF)
             att[part] = whole
             normed[part] = layer_norm(whole.astype(F32))
         return 0
@@ -374,26 +480,31 @@
     lax.fori_loop(0, 8, up_one, 0)
     pump("down0")
 
-    def down_one(b):
-        mine, other, _, _, off, edge, _ = geometry(b)
-        rows = pl.ds(b * 256, 256)
-        got = jnp.dot(hid[rows], wd[...].reshape(4 * D, D), preferred_element_type=F32)
-        got = got + att[rows].astype(F32)
-        for j in range(5):
-            left = got[64 * max(j - 1, 0) : 64 * max(j - 1, 0) + 64]
-            right = got[64 * min(j, 3) : 64 * min(j, 3) + 64]
-            whole = jnp.where(early, left, right).astype(BF).reshape(8, 8, D)
-            back[b, :, j] = whole
-            if j != edge:
-                out[b, mine, j - off] = whole[4:] if b < 2 else whole[:4]
-        for c in returns(b):
-            c.start()
-
-    for b in (0, 2, 1, 3):
-        down_one(b)
+    def down_one(i):
+        half = i // 2
+        got = jnp.dot(hid[256 * i : 256 * i + 256], wd[...].reshape(4 * D, D), preferred_element_type=F32)
+        got = got + att[256 * i : 256 * i + 256].astype(F32)
+        for b in (2 * (i % 2), 2 * (i % 2) + 1):
+            mine, other, _, _, off, edge, _ = geometry(b)
+            base = 128 * (b % 2)
+            for j in range(5):
+                left = got[base + 32 * max(j - 1, 0) : base + 32 * max(j - 1, 0) + 32]
+                right = got[base + 32 * min(j, 3) : base + 32 * min(j, 3) + 32]
+                whole = jnp.where(early, left, right).astype(BF).reshape(4, 8, D)
+                if half == 1:
+                    back[b, other, j] = whole
+                elif j == edge:
+                    back[b, mine, j] = whole
+                else:
+                    out[b, mine, j - off] = whole
+            for k in (0, 2) if half == 1 else (1,):
+                returns(b)[k].start()
+
+    for i in (2, 3, 0, 1):
+        down_one(i)
 
     early_cols = lax.broadcasted_iota(jnp.int32, (64, D), 0) % 8 < 4
-    for b in (0, 2, 1, 3):
+    for b in range(4):
         border = geometry(b)[6]
         for c in returns(b):
             c.wait_recv()
@@ -410,32 +521,7 @@
             c.wait_send()
 
 
-def window_order(values):
-    return jnp.roll(values, (4, 4), axis=(-2, -1)).reshape(values.shape[:-2] + (64,))
-
-
 def per_device(tokens, qkv_weight, proj_weight, up_weight, down_weight, bias_table, sea_mask):
-    head_count = bias_table.shape[1]
-    lat = lax.axis_index("lat")
-    lon = lax.axis_index("lon")
-
-    cells = window_order(jnp.arange(64, dtype=jnp.int32).reshape(8, 8))
-    row_of, col_of = cells // 8, cells % 8
-    offsets = (row_of[:, None] - row_of[None, :] + 7) * 15 + (col_of[:, None] - col_of[None, :] + 7)
-    one_hot = (offsets.reshape(-1)[:, None] == jnp.arange(bias_table.shape[0], dtype=jnp.int32)).astype(F32)
-    bias = jnp.dot(one_hot, bias_table, precision=lax.Precision.HIGHEST)
-    bias = bias.reshape(64, 64, head_count // 4, 4).transpose(2, 0, 3, 1).reshape(head_count // 4, 64, 256)
-
-    around = jnp.pad(sea_mask, ((8, 16), (8, 16)), mode="wrap")
-    rows = []
-    for b in range(4):
-        r0 = 8 * (lat if b < 2 else lat - 1) + 8 + 4
-        c0 = 32 * lon - (0 if b % 2 == 0 else 8) + 8 + 4
-        cut = lax.dynamic_slice(around, (r0, c0), (8, 32))
-        rows.append(window_order(cut.reshape(8, 4, 8).transpose(1, 0, 2)))
-    keys = jnp.where(jnp.concatenate(rows, axis=0) == 1, 0.0, FAR).astype(F32)
-    keys = jnp.concatenate([keys, keys], axis=1)
-
     hbm = pl.BlockSpec(memory_space=pl.ANY)
     vmem = pl.BlockSpec(memory_space=pltpu.VMEM)
     shard = (2, 4, 2, 2, 4)
@@ -459,6 +545,9 @@
             pltpu.VMEM((1024, 4 * D), BF),
             pltpu.VMEM((4, 8, 5, 8, D), BF),
             pltpu.VMEM((4, 8, 8, D), BF),
+            pltpu.VMEM((4, 15, 16, 256), F32),
+            pltpu.VMEM((4, 64, 256), F32),
+            pltpu.VMEM((16, 128), F32),
             dma((messages,)),
             dma((messages,)),
             dma((4,)),
@@ -472,7 +561,7 @@
             collective_id=0, has_side_effects=True, vmem_limit_bytes=67043328
         ),
         name="swin_block",
-    )(tokens.reshape(tile), qkv_weight, proj_weight, up_weight, down_weight, bias, keys)
+    )(tokens.reshape(tile), qkv_weight, proj_weight, up_weight, down_weight, bias_table, sea_mask)
     return out.reshape(tokens.shape)
 
 

time: 136 us -> 118 us (0.87)
  Pallas kernels: 122 us -> 113 us
  other arithmetic: 3.49 us -> 0 us
  local copies, waits for them, and re-layouts: 7.34 us -> 4.65 us
  matrix products: 2.56 us -> 0 us
    pallas_call x1, Pallas kernels: 122 us -> 113 us  [per_device(): pl.pallas_call(block_kernel, out_shape=jax.ShapeDtypeStruct(tile, BF), in...]
    concatenate x13 -> x0, other arithmetic: 3.38 us -> none  [the longest x2 1.97 us: per_device(): around = jnp.pad(sea_mask, ((8, 16), (8, 16)), mode='wrap')]
    dot_general x1 -> x0, matrix products: 2.56 us -> none  [per_device(): bias = jnp.dot(one_hot, bias_table, precision=lax.Precision.HIGHEST)]
    reshape x12 -> x0, local copies, waits for them, and re-layouts: 2.34 us -> none  [the longest x3 1.62 us: per_device(): bias.reshape(64, 64, head_count // 4, 4).transpose(2, 0, 3, 1)]
    slice x10 -> x0, local copies, waits for them, and re-layouts: 1.61 us -> none  [the longest x4 1.51 us: per_device(): around = jnp.pad(sea_mask, ((8, 16), (8, 16)), mode='wrap')]
    unnamed x3 -> x2, local copies, waits for them, and re-layouts: 3.19 us -> 4.65 us
where the time goes in v2:
time: 118 us; the launch traced here: 117 us
  Pallas kernels  113 us (96%)
  local copies, waits for them, and re-layouts  4.65 us (4%)
    pallas_call x1, Pallas kernels, per_device(): pl.pallas_call(block_kernel, out_shape=jax.ShapeDtypeStruct(tile, BF), in...  113 us
    unnamed x2, local copies, waits for them, and re-layouts  4.65 us

profile of v2, /device:TPU:1, one launch (start us, length us, event | category | flops | bytes accessed | tf_op | source)
XLA Modules:
  0.0 117.2 jit_solution(1273818659895040402)
XLA Ops:
  0.0 1.5 %copy.8.table = f32[225,16]{1,0:T(8,128)} copy(f32[225,16]{0,1:T(8,128)} %param.12) | data formatting | bytes 28800 | tf_op args[5]
  1.5 112.5 %swin_block.1 = bf16[4,8,4,8,1024]{4,3,2,1,0:T(8,128)(2,1)} custom-call(bf16[4,8,4,8,1024]{4,3,2,1,0:T(8,128)(2,1)} %bitcast.3, bf16[24,1024]{1,0:T(8,128)(2,1)} %wq_in.1, bf16[8,1024]{1,0:T(8,128)(2,1)} %wp_in.1, bf16[32,1024]{1,0:T(8,128)(2,1)} %wu_in.1, bf16[32,1024]{1,0:T(8,128)(2,1)} %wd_in.1, f32[225,16]{1,0:T(8,128)} %copy.8.table, s32[128,256]{1,0:T(8,128)} %sea.1), custom_call_target="tpu_custom_call" | custom-call | tf_op jit(solution)/shard_map/swin_block/pallas_call | solution.py:531
  114.0 3.2 %copy.10 = bf16[4,8,32,1024]{3,2,1,0:T(8,128)(2,1)} copy(bf16[4,8,32,1024]{3,2,1,0:T(8,128)(2,1)} %bitcast.2) | data formatting | bytes 4194304

commit v3 on v2

v3 whole, which is shorter than its diff:
```python
import jax
import jax.numpy as jnp
from jax import lax
from jax.experimental import pallas as pl
from jax.experimental.pallas import tpu as pltpu
from jax.sharding import PartitionSpec as P

MESH = pl.DeviceIdType.MESH
BF = jnp.bfloat16
F32 = jnp.float32
D = 1024
FAR = -1e30

PIECES = {
    "qa": (0, 0, 0, 1024, "xyz"),
    "qb": (0, 8, 0, 1024, "yzx"),
    "qc": (0, 16, 0, 1024, "zxy"),
    "p": (1, 0, 0, 1024, "xyz"),
    "c0a": (2, 0, 0, 384, "yzx"),
    "c0b": (2, 0, 384, 384, "zxy"),
    "c0c": (2, 0, 768, 256, "xyz"),
    "c1a": (2, 1, 0, 384, "yzx"),
    "c1b": (2, 1, 384, 384, "zxy"),
    "c1c": (2, 1, 768, 256, "xyz"),
    "c2a": (2, 2, 0, 384, "yzx"),
    "c2b": (2, 2, 384, 384, "zxy"),
    "c2c": (2, 2, 768, 256, "xyz"),
    "c3a": (2, 3, 0, 384, "yzx"),
    "c3b": (2, 3, 384, 384, "zxy"),
    "c3c": (2, 3, 768, 256, "xyz"),
}
NAMES = list(PIECES)
FINE = ("qa", "qb", "qc")
COUNT = {n: 27 if n in FINE else 15 for n in NAMES}
START = {n: sum(COUNT[m] for m in NAMES[:k]) for k, n in enumerate(NAMES)}
FINE_STEPS = {
    1: ((), (0, 1, 2)),
    2: ((0, 1, 2), (3, 4, 7, 8)),
    3: ((3, 4), (5, 6, 11, 12, 15, 16)),
    4: ((5, 6), (19, 20, 23)),
    5: ((7, 8), (9, 10)),
    6: ((11, 12, 15, 16), (13, 14, 17, 18)),
    7: ((19, 20), (21, 22, 24, 25)),
    8: ((9, 10, 13, 14, 17, 18, 21, 22), (26,)),
    9: ((23, 24, 25, 26), ()),
}
STEPS = {
    1: ((), (0, 1, 2)),
    2: ((0, 1, 2), (3, 4)),
    3: ((3, 4), (5, 6)),
    4: ((5, 6), (7, 8, 11)),
    5: ((7, 8), (9, 10, 12, 13)),
    6: ((9, 10), (14,)),
    7: ((11, 12, 13, 14), ()),
}
PLAN = [
    ("start", 1, "qa"),
    ("start", 1, "qb"),
    ("start", 1, "qc"),
    ("start", "halo", 1),
    ("start", "halo", 3),
    ("start", "halo", 5),
    ("normA", 2, "qa"),
    ("normA", 2, "qb"),
    ("normA", 2, "qc"),
    ("normA", "halo", 4),
    ("normA", "halo", 0),
    ("normA", "halo", 2),
    ("normA", 3, "qa"),
    ("normA", 3, "qb"),
    ("normA", 3, "qc"),
    ("normA", 1, "p"),
    ("normA", 1, "c0a"),
    ("normA", 1, "c0b"),
    ("normA", 1, "c0c"),
    ("normA", 1, "c1a"),
    ("normA", 1, "c1b"),
    ("normA", 1, "c1c"),
    ("normA", 1, "c2a"),
    ("normA", 1, "c2b"),
    ("normA", 1, "c2c"),
    ("normA", 1, "c3a"),
    ("normA", 1, "c3b"),
    ("normA", 1, "c3c"),
    ("normB", 4, "qa"),
    ("normB", 5, "qa"),
    ("normB", 6, "qa"),
    ("qkv0", 4, "qb"),
    ("qkv0", 4, "qc"),
    ("qkv0", 2, "c0b"),
    ("qkv0", 5, "qb"),
    ("qkv0", 5, "qc"),
    ("qkv0", 6, "qb"),
    ("qkv0", 6, "qc"),
    ("qkv0", 2, "c1b"),
    ("qkv0", 2, "p"),
    ("qkv0", 2, "c0a"),
    ("qkv0", 2, "c2b"),
    ("qkv0", 2, "c0c"),
    ("qkv0", 2, "c1a"),
    ("qkv0", 2, "c1c"),
    ("qkv0", 2, "c3b"),
    ("qkv0", 2, "c2c"),
    ("qkv0", 2, "c2a"),
    ("qkv0", 7, "qa"),
    ("qkv0", 2, "c3c"),
    ("qkv0", 2, "c3a"),
    ("qkv0", 7, "qb"),
    ("qkv0", 7, "qc"),
    ("qkv0", 3, "c0b"),
    ("qkv0", 3, "c0a"),
    ("qkv0", 3, "c1a"),
    ("qkv0", 3, "p"),
    ("qkv0", 3, "c2a"),
    ("qkv0", 3, "c1b"),
    ("qkv0", 3, "c0c"),
    ("qkv0", 8, "qa"),
    ("qkv0", 3, "c1c"),
    ("qkv0", 3, "c2b"),
    ("qkv0", 3, "c3a"),
    ("qkv0", 3, "c2c"),
    ("qkv0", 4, "c0a"),
    ("qkv0", 9, "qa"),
    ("qkv0", 3, "c3b"),
    ("qkv0", 3, "c3c"),
    ("qkv0", 4, "c1a"),
    ("qkv0", 8, "qb"),
    ("qkv0", 8, "qc"),
    ("qkv0", 4, "c0b"),
    ("qkv0", 4, "p"),
    ("qkv0", 4, "c1b"),
    ("qkv0", 4, "c0c"),
    ("qkv0", 9, "qb"),
    ("qkv0", 9, "qc"),
    ("qkv3", 5, "c0a"),
    ("qkv3", 4, "c2a"),
    ("att0", 5, "c0b"),
    ("att0", 4, "c2b"),
    ("att1", 5, "p"),
    ("att1", 4, "c1c"),
    ("att3", 5, "c1a"),
    ("att3", 4, "c3a"),
    ("att5", 5, "c1b"),
    ("att5", 4, "c3b"),
    ("att5", 5, "c0c"),
    ("att5", 4, "c2c"),
    ("att7", 6, "c0a"),
    ("att9", 6, "c0b"),
    ("att11", 7, "c0a"),
    ("att12", 6, "p"),
    ("att13", 7, "c0b"),
    ("att14", 5, "c2a"),
    ("proj0", 7, "p"),
    ("proj0", 5, "c1c"),
    ("proj0", 4, "c3c"),
    ("proj0", 5, "c2b"),
    ("proj1", 6, "c1a"),
    ("proj2", 6, "c0c"),
    ("proj2", 6, "c1b"),
    ("proj3", 7, "c1a"),
    ("big0", 7, "c0c"),
    ("big0", 7, "c1b"),
    ("big0", 5, "c2c"),
    ("big1", 6, "c1c"),
    ("big1", 6, "c2a"),
    ("big1", 5, "c3a"),
    ("big1", 5, "c3b"),
    ("big1", 5, "c3c"),
    ("big1", 6, "c2b"),
    ("big1", 7, "c1c"),
    ("big2", 7, "c2a"),
    ("big2", 7, "c2b"),
    ("big2", 6, "c2c"),
    ("big2", 6, "c3c"),
    ("big2", 6, "c3a"),
    ("big2", 6, "c3b"),
    ("big2", 7, "c2c"),
    ("big3", 7, "c3a"),
    ("big3", 7, "c3b"),
    ("big3", 7, "c3c"),
]


def planned(slot):
    return [(what, name) for where, what, name in PLAN if where == slot]


def block_kernel(
    tok, wq_in, wp_in, wu_in, wd_in, table, sea,
    out, side,
    wq, wp, wf, ext, normed, qkv, att, acc, back, spread, bias, keys,
    w_send, w_recv, own_sem, h_send, h_recv, r_send, r_recv, t_sem, o_sem,
):
    lat = lax.axis_index("lat")
    lon = lax.axis_index("lon")
    core = lat % 2
    y = (lat // 2) % 4
    z_lo = lat // 8
    x = lon % 4
    z_hi = lon // 4
    at = {"x": x, "y": y, "z": z_hi * 2 + z_lo}

    def device(over, partner=False):
        c = dict(at)
        c.update(over)
        k = 1 - core if partner else core
        return {"lat": ((c["z"] % 2) * 4 + c["y"]) * 2 + k, "lon": (c["z"] // 2) * 4 + c["x"]}

    ring = {a: [at[a]] + [(at[a] + by) % 4 for by in (1, 2, 3)] for a in "xyz"}

    def near(axis, by):
        return ring[axis][by % 4]

    def shifted(d_lat, d_lon):
        return {"lat": (lat + d_lat + 16) % 16, "lon": (lon + d_lon + 8) % 8}

    held = (wq, wp, wf)

    def region(name, c, where):
        which, first, col, cols, _ = PIECES[name]
        ref = held[which]

        def part(axis):
            v = where[axis]
            if v is None:
                return slice(None)
            if isinstance(v, tuple):
                return pl.ds(2 * v[1], 2)
            return v

        v = where["z"]
        if v is None:
            lo, hi = slice(None), slice(None)
        elif isinstance(v, tuple):
            lo, hi = v[1], slice(None)
        else:
            lo, hi = v % 2, v // 2
        rows = (first, slice(None)) if which == 2 else (pl.ds(first, 8),)
        return ref.at[(lo, part("y"), c, hi, part("x"), *rows, pl.ds(col, cols))]

    targets = {(a, by): device({a: near(a, by)}) for a in "xyz" for by in (1, 2, 3)}
    partner = device({}, True)

    def message(name, m):
        a1, a2, a3 = PIECES[name][4]
        here = dict(at)
        if m < 3:
            by = (1, 3, 2)[m]
            return here, {**here, a1: near(a1, -by)}, targets[a1, by]
        m -= 3
        line = {**here, a1: None}
        plane = {**line, a2: None}
        if m < 4:
            axis, whole = a2, line
        elif name in FINE and m < 20:
            axis, whole = a3, {**line, a2: near(a2, (0, 3, 1, 2)[(m - 4) // 4])}
        elif m < 8:
            axis, whole = a3, plane
        else:
            by = (0, 1, 3, 2)[m - (20 if name in FINE else 8)]
            sent = {**plane, a3: near(a3, by)}
            return sent, sent, partner
        m %= 4
        if m < 2:
            by = 1 if m == 0 else 3
            return whole, {**whole, axis: near(axis, -by)}, targets[axis, by]
        by = 1 if m == 2 else 3
        half = {**whole, a1: ("h", m - 2)}
        return {**half, axis: near(axis, -by)}, {**half, axis: near(axis, 2)}, targets[axis, by]

    def weight_copy(name, m, where, to):
        k = START[name] + m
        there = region(name, core, where)
        return pltpu.make_async_remote_copy(
            src_ref=there, dst_ref=there, send_sem=w_send.at[k], recv_sem=w_recv.at[k],
            device_id=to, device_id_type=MESH,
        )

    def send(name, m):
        sent, _, to = message(name, m)
        return weight_copy(name, m, sent, to)

    def came(name, m):
        _, landed, to = message(name, m)
        return weight_copy(name, m, landed, to)

    def step(number, name):
        awaited, sent = (FINE_STEPS if name in FINE else STEPS)[number]
        for m in awaited:
            came(name, m).wait_recv()
        for m in sent:
            send(name, m).start()

    def pump(slot):
        for what, name in planned(slot):
            if what == "halo":
                for b in (0, 2, 1, 3):
                    halo(b, name).start()
            else:
                step(what, name)

    def pump_at(prefix, i, count):
        for k in range(count):
            if planned(f"{prefix}{k}"):
                @pl.when(i == (k - k % 2 if prefix == "att" else k))
                def _(k=k):
                    pump(f"{prefix}{k}")

    def geometry(b):
        ahead = b < 2
        right = b % 2 == 0
        mine = pl.ds(4, 4) if ahead else pl.ds(0, 4)
        other = pl.ds(0, 4) if ahead else pl.ds(4, 4)
        d_lat = 1 if ahead else -1
        d_lon = 1 if right else -1
        off = 0 if right else 1
        edge = 4 if right else 0
        border = 0 if right else 3
        return mine, other, d_lat, d_lon, off, edge, border

    def halo(b, k):
        _, other, d_lat, d_lon, off, edge, border = geometry(b)
        mine_first, other_first = (4, 0) if b < 2 else (0, 4)
        mine = pl.ds(mine_first, 4)
        if k < 4:
            src, dst = tok.at[b, other_first + k], ext.at[b, other_first + k, pl.ds(off, 4)]
            to = shifted(-d_lat, 0)
        elif k == 4:
            src, dst, to = tok.at[b, mine, border], ext.at[b, mine, edge], shifted(0, -d_lon)
        else:
            src, dst, to = tok.at[b, other, border], ext.at[b, other, edge], shifted(-d_lat, -d_lon)
        return pltpu.make_async_remote_copy(
            src_ref=src, dst_ref=dst, send_sem=h_send.at[6 * b + k], recv_sem=h_recv.at[6 * b + k],
            device_id=to, device_id_type=MESH,
        )

    def local_tokens(b):
        mine, _, _, _, off, _, _ = geometry(b)
        return pltpu.make_async_copy(tok.at[b, mine], ext.at[b, mine, pl.ds(off, 4)], t_sem.at[b])

    def returns(b, k):
        mine, other, d_lat, d_lon, off, edge, _ = geometry(b)
        src, dst, to = (
            (back.at[b, other, pl.ds(off, 4)], out.at[b, other], (d_lat, 0)),
            (back.at[b, mine, edge], side.at[b, mine], (0, d_lon)),
            (back.at[b, other, edge], side.at[b, other], (d_lat, d_lon)),
        )[k]
        return pltpu.make_async_remote_copy(
            src_ref=src, dst_ref=dst, send_sem=r_send.at[3 * b + k], recv_sem=r_recv.at[3 * b + k],
            device_id=shifted(*to), device_id_type=MESH,
        )

    def own(which):
        here = (z_lo, y, core, z_hi, x)
        src, dst = (
            (wq_in, wq.at[here]),
            (wp_in, wp.at[here]),
            (wu_in, wf.at[(*here, slice(None), pl.ds(0, 8))]),
            (wd_in, wf.at[(*here, slice(None), pl.ds(8, 8))]),
        )[which]
        return pltpu.make_async_copy(src, dst, own_sem.at[which])

    for which in range(4):
        own(which).start()
    for b in range(4):
        local_tokens(b).start()

    barrier = pltpu.get_barrier_semaphore()
    peers = list(targets.values()) + [partner]
    peers += [shifted(i, j) for i in (-1, 0, 1) for j in (-1, 0, 1) if (i, j) != (0, 0)]
    for peer in peers:
        pl.semaphore_signal(barrier, inc=1, device_id=peer, device_id_type=MESH)
    pl.semaphore_wait(barrier, len(peers))

    for which in range(4):
        own(which).wait()
    pump("start")

    pump("keys")
    spot = lax.broadcasted_iota(jnp.int32, (256, 512), 1)
    spot_col = spot % 8
    spot_window = spot // 128
    grid_col = lax.broadcasted_iota(jnp.int32, (256, 512), 0)
    own_row = lax.broadcasted_iota(jnp.int32, (8, 512), 0) == (lax.broadcasted_iota(jnp.int32, (8, 512), 1) // 8) % 8
    for b in range(4):
        row = lat if b < 2 else (lat + 15) % 16
        block = lon * 4 + (0 if b % 2 == 0 else 31)
        upper = sea[pl.ds(pl.multiple_of(row * 8, 8), 8)]
        lower = sea[pl.ds(pl.multiple_of(((row + 1) % 16) * 8, 8), 8)]
        band = jnp.concatenate([upper[4:], lower[:4]], axis=0)
        open_at = jnp.where(band == 1, 1.0, 0.0).astype(BF)
        wanted = ((block + spot_window + jnp.where(spot_col < 4, 1, 0)) * 8 + spot_col) % 256
        chosen = jnp.where(grid_col == wanted, 1.0, 0.0).astype(BF)
        found = jnp.dot(open_at, chosen, preferred_element_type=F32)
        found = jnp.sum(jnp.where(own_row, found, 0.0), axis=0, keepdims=True)
        closed = jnp.where(found > 0.5, 0.0, FAR)
        for w in range(4):
            keys[4 * b + w : 4 * b + w + 1] = closed[:, 128 * w : 128 * w + 128]

    pump("bias")
    lane = lax.broadcasted_iota(jnp.int32, (16, 256), 1)
    head_row = lax.broadcasted_iota(jnp.int32, (16, 256), 0)
    lane_row = (lane % 64) // 8
    col_step = (lax.broadcasted_iota(jnp.int32, (8, 256), 0) + 4) % 8 - (
        lax.broadcasted_iota(jnp.int32, (8, 256), 1) + 4
    ) % 8 + 7
    for g in range(4):
        over_lanes = jnp.where(head_row == 4 * g + lane // 64, 1.0, 0.0)
        wide = jnp.dot(
            table[...], over_lanes, precision=lax.Precision.HIGHEST, preferred_element_type=F32
        )
        for d in range(15):
            spread[g, d, 0:15] = wide[15 * d : 15 * d + 15]

    def bias_one(i, _):
        g, r = i // 8, i % 8
        steps = jnp.zeros((16, 256), F32)
        for k in range(8):
            steps = jnp.where(lane_row == k, spread[g, r - k + 7], steps)
        line = jnp.zeros((8, 256), F32)
        for d in range(15):
            line = jnp.where(col_step == d, steps[d : d + 1], line)
        bias[g, pl.ds(pl.multiple_of(r * 8, 8), 8)] = line
        return 0

    lax.fori_loop(0, 32, bias_one, 0)

    def other_row(b, w):
        return 512 + 128 * ((b + 2 * core) % 4) + 32 * w

    def own_row(b, w):
        if isinstance(b, int):
            edge_here = w == (3 if b % 2 == 0 else 0)
            return 384 + 32 * b if edge_here else 32 * (3 * b + w - b % 2)
        odd = b % 2
        edge_here = w == 3 - 3 * odd
        return jnp.where(edge_here, 384 + 32 * b, 32 * (3 * b + w - odd))

    early = lax.broadcasted_iota(jnp.int32, (32, D), 0) % 8 < 4

    def window_half(b, w, half):
        rows = pl.ds(jnp.where((b < 2) == (half == 0), 4, 0), 4)
        left = ext[b, rows, w].astype(F32).reshape(32, D)
        right = ext[b, rows, w + 1].astype(F32).reshape(32, D)
        return jnp.where(early, right, left)

    def layer_norm(v):
        centre = jnp.mean(v, axis=-1, keepdims=True)
        moved = v - centre
        spread_of = jnp.mean(moved * moved, axis=-1, keepdims=True)
        return (moved * lax.rsqrt(spread_of + 1e-05)).astype(BF)

    def norm_half(half):
        def norm_one(i, _):
            first = (other_row if half else own_row)(i // 4, i % 4)
            rows = pl.ds(pl.multiple_of(first, 32), 32)
            normed[rows] = layer_norm(window_half(i // 4, i % 4, half))
            return 0

        lax.fori_loop(0, 16, norm_one, 0)

    pump("normA")
    for b in range(4):
        local_tokens(b).wait()
        halo(b, 4).wait_recv()
    norm_half(0)
    pump("normB")
    for b in range(4):
        for k in (0, 1, 2, 3, 5):
            halo(b, k).wait_recv()
    norm_half(1)

    def qkv_one(i, _):
        pump_at("qkv", i, 4)
        w = wq[i // 2, pl.ds((i % 2) * 2, 2)].reshape(768, D)
        got = lax.dot_general(normed[...], w, (((1,), (1,)), ((), ())), preferred_element_type=F32)
        qkv[:, pl.ds(pl.multiple_of(i * 768, 768), 768)] = got.astype(BF)
        return 0

    lax.fori_loop(0, 4, qkv_one, 0)

    lane_head = lax.broadcasted_iota(jnp.int32, (64, 256), 1) // 64
    pick = [lane_head == h for h in range(4)]
    ones_at = (
        lax.broadcasted_iota(jnp.int32, (256, 256), 0) // 64
        == lax.broadcasted_iota(jnp.int32, (256, 256), 1) // 64
    )
    ones = jnp.where(ones_at, 1.0, 0.0).astype(BF)
    first_half = lax.broadcasted_iota(jnp.int32, (64, 128), 1) < 64
    q_cell = lax.broadcasted_iota(jnp.int32, (64, 128), 0)
    k_cell = lax.broadcasted_iota(jnp.int32, (64, 128), 1) % 64
    itself = q_cell == k_cell
    parted = (q_cell < 32) != (k_cell < 32)

    def spread_heads(v):
        wide = v.astype(F32)
        return jnp.concatenate([jnp.where(p, wide, 0.0).astype(BF) for p in pick], axis=0)

    def attend_one(i, _):
        owned, foreign = own_row(i // 4, i % 4), other_row(i // 4, i % 4)
        top = pl.ds(pl.multiple_of(jnp.where(i < 8, owned, foreign), 32), 32)
        low = pl.ds(pl.multiple_of(jnp.where(i < 8, foreign, owned), 32), 32)

        def cut(first):
            return jnp.concatenate([qkv[top, pl.ds(first, 256)], qkv[low, pl.ds(first, 256)]], axis=0)

        at_end = jnp.where(i < 8, lat, (lat + 15) % 16) == 15
        end_value = jnp.where(at_end, FAR, 0.0)
        mask = jnp.where(itself, 0.0, jnp.broadcast_to(keys[pl.ds(i, 1)], (64, 128)))
        mask = jnp.where(parted, mask + end_value, mask)
        for g in range(4):
            q, k, v = cut(256 * g), cut(D + 256 * g), cut(2 * D + 256 * g)
            scores = lax.dot_general(
                q, spread_heads(k), (((1,), (1,)), ((), ())), preferred_element_type=F32
            )
            weights = []
            for t in range(2):
                s = scores[:, 128 * t : 128 * t + 128] * 0.125 + bias[g, :, pl.ds(128 * t, 128)] + mask
                top_a = jnp.max(jnp.where(first_half, s, -jnp.inf), axis=1, keepdims=True)
                top_b = jnp.max(jnp.where(first_half, -jnp.inf, s), axis=1, keepdims=True)
                weights.append(jnp.exp(s - jnp.where(first_half, top_a, top_b)).astype(BF))
            e = jnp.concatenate(weights, axis=1)
            total = jnp.dot(e, ones, preferred_element_type=F32)
            context = jnp.dot(e, spread_heads(v), preferred_element_type=F32) / total
            att[top, pl.ds(256 * g, 256)] = context[:32].astype(BF)
            att[low, pl.ds(256 * g, 256)] = context[32:].astype(BF)
        return 0

    def attend_two(i, _):
        pump_at("att", i * 2, 16)
        attend_one(i * 2, 0)
        attend_one(i * 2 + 1, 0)
        return 0

    lax.fori_loop(0, 8, attend_two, 0)

    def proj_one(i, _):
        pump_at("proj", i, 4)
        rows = pl.ds(pl.multiple_of(i * 256, 256), 256)
        got = lax.dot_general(
            att[rows], wp[...].reshape(D, D), (((1,), (1,)), ((), ())), preferred_element_type=F32
        )
        for w in range(8):
            part = pl.ds(pl.multiple_of(i * 256 + w * 32, 32), 32)
            slot = i * 8 + w
            edge_b = jnp.clip(slot - 12, 0, 3)
            inner_b = jnp.minimum(slot // 3, 3)
            b = jnp.where(slot < 12, inner_b, jnp.where(slot < 16, edge_b, (slot // 4 + 2 * core) % 4))
            inner_w = jnp.minimum(slot % 3 + inner_b % 2, 3)
            at_w = jnp.where(slot < 12, inner_w, jnp.where(slot < 16, 3 - 3 * (edge_b % 2), slot % 4))
            before = window_half(b, at_w, i // 2)
            whole = (before + got[32 * w : 32 * w + 32]).astype(BF)
            acc[part] = whole.astype(F32)
            normed[part] = layer_norm(whole.astype(F32))
        return 0

    lax.fori_loop(0, 4, proj_one, 0)

    def feed(rows, k):
        up = wf[:, :, :, :, :, k, pl.ds(0, 8)].reshape(D, D)
        hidden = lax.dot_general(normed[rows], up, (((1,), (1,)), ((), ())), preferred_element_type=F32)
        hidden = jax.nn.gelu(hidden).astype(BF)
        down = wf[:, :, :, :, :, k, pl.ds(8, 8)].reshape(D, D)
        acc[rows] += jnp.dot(hidden, down, preferred_element_type=F32)

    def feed_sent(k, _):
        pump_at("big", k, 3)
        feed(pl.ds(384, 640), k)
        return 0

    def feed_kept(k, _):
        feed(pl.ds(0, 384), k)
        return 0

    def finish_other(samples):
        for b in samples:
            mine, other, _, _, _, edge, _ = geometry(b)
            for j in range(5):
                left = acc[pl.ds(pl.multiple_of(other_row(b, max(j - 1, 0)), 32), 32)]
                right = acc[pl.ds(pl.multiple_of(other_row(b, min(j, 3)), 32), 32)]
                back[b, other, j] = jnp.where(early, left, right).astype(BF).reshape(4, 8, D)
        for b in samples:
            returns(b, 0).start()
            returns(b, 2).start()

    lax.fori_loop(0, 3, feed_sent, 0)
    pump("big3")
    feed(pl.ds(768, 256), 3)
    pl.when(core == 1)(lambda: finish_other((0, 1)))
    pl.when(core == 0)(lambda: finish_other((2, 3)))
    feed(pl.ds(384, 384), 3)
    for b in range(4):
        mine, _, _, _, _, edge, _ = geometry(b)
        back[b, mine, edge] = acc[pl.ds(384 + 32 * b, 32)].astype(BF).reshape(4, 8, D)
        returns(b, 1).start()
    pl.when(core == 1)(lambda: finish_other((2, 3)))
    pl.when(core == 0)(lambda: finish_other((0, 1)))

    lax.fori_loop(0, 4, feed_kept, 0)

    def keep(b):
        mine, _, _, _, off, _, _ = geometry(b)
        return pltpu.make_async_copy(back.at[b, mine, pl.ds(off, 4)], out.at[b, mine], o_sem.at[b])

    for b in range(4):
        mine, _, _, _, _, edge, _ = geometry(b)
        for j in range(5):
            if j != edge:
                left = acc[pl.ds(own_row(b, max(j - 1, 0)), 32)]
                right = acc[pl.ds(own_row(b, min(j, 3)), 32)]
                back[b, mine, j] = jnp.where(early, left, right).astype(BF).reshape(4, 8, D)
        keep(b).start()
    for b in range(4):
        keep(b).wait()
        for k in range(3):
            returns(b, k).wait_recv()

    for n in NAMES:
        for m in range(COUNT[n]):
            send(n, m).wait_send()
    for b in range(4):
        for k in range(6):
            halo(b, k).wait_send()
        for k in range(3):
            returns(b, k).wait_send()


def merge_kernel(got, side, out):
    out[...] = got[...]
    late = lax.broadcasted_iota(jnp.int32, (64, D), 0) % 8 >= 4
    from_side = side[...].astype(F32).reshape(64, D)
    odd = pl.program_id(0) % 2 == 1

    @pl.when(jnp.logical_not(odd))
    def _():
        here = got[0, :, 0].astype(F32).reshape(64, D)
        out[0, :, 0] = jnp.where(late, here, from_side).astype(BF).reshape(8, 8, D)

    @pl.when(odd)
    def _():
        here = got[0, :, 3].astype(F32).reshape(64, D)
        out[0, :, 3] = jnp.where(late, from_side, here).astype(BF).reshape(8, 8, D)


def per_device(tokens, qkv_weight, proj_weight, up_weight, down_weight, bias_table, sea_mask):
    hbm = pl.BlockSpec(memory_space=pl.ANY)
    vmem = pl.BlockSpec(memory_space=pltpu.VMEM)
    shard = (2, 4, 2, 2, 4)
    tile = (4, 8, 4, 8, D)
    messages = sum(COUNT.values())
    dma = pltpu.SemaphoreType.DMA
    got, side = pl.pallas_call(
        block_kernel,
        out_shape=(jax.ShapeDtypeStruct(tile, BF), jax.ShapeDtypeStruct((4, 8, 8, D), BF)),
        in_specs=[hbm] * 5 + [vmem, vmem],
        out_specs=(hbm, hbm),
        scratch_shapes=[
            pltpu.VMEM(shard + (24, D), BF),
            pltpu.VMEM(shard + (8, D), BF),
            pltpu.VMEM(shard + (4, 16, D), BF),
            pltpu.VMEM((4, 8, 5, 8, D), BF),
            pltpu.VMEM((1024, D), BF),
            pltpu.VMEM((1024, 3 * D), BF),
            pltpu.VMEM((1024, D), BF),
            pltpu.VMEM((1024, D), F32),
            pltpu.VMEM((4, 8, 5, 8, D), BF),
            pltpu.VMEM((4, 15, 16, 256), F32),
            pltpu.VMEM((4, 64, 256), F32),
            pltpu.VMEM((16, 128), F32),
            dma((messages,)),
            dma((messages,)),
            dma((4,)),
            dma((24,)),
            dma((24,)),
            dma((12,)),
            dma((12,)),
            dma((4,)),
            dma((4,)),
        ],
        compiler_params=pltpu.CompilerParams(
            collective_id=0, has_side_effects=True, vmem_limit_bytes=67043328
        ),
        name="swin_block",
    )(
        tokens.reshape(tile), qkv_weight, proj_weight, up_weight.reshape(4, 8, D), down_weight.reshape(4, 8, D),
        bias_table, sea_mask,
    )
    out = pl.pallas_call(
        merge_kernel,
        grid=(4,),
        out_shape=jax.ShapeDtypeStruct(tile, BF),
        in_specs=[
            pl.BlockSpec((1, 8, 4, 8, D), lambda b: (b, 0, 0, 0, 0)),
            pl.BlockSpec((1, 8, 8, D), lambda b: (b, 0, 0, 0)),
        ],
        out_specs=pl.BlockSpec((1, 8, 4, 8, D), lambda b: (b, 0, 0, 0, 0)),
        name="merge_borders",
    )(got, side)
    return out.reshape(tokens.shape)


def solution(mesh):
    placed = (
        P(None, "lat", "lon", None),
        P(("lat", "lon"), None),
        P(("lat", "lon"), None),
        P(("lat", "lon"), None),
        P(("lat", "lon"), None),
        P(),
        P(),
    )
    return jax.shard_map(
        per_device,
        mesh=mesh,
        in_specs=placed,
        out_specs=P(None, "lat", "lon", None),
        check_vma=False,
    )
```

time: 118 us -> 106 us (0.90)
  Pallas kernels: 113 us -> 104 us
  local copies, waits for them, and re-layouts: 4.65 us -> 1.46 us
    pallas_call x1 -> x2, Pallas kernels: 113 us -> 104 us  [the longest x1 100 us: per_device(): pl.pallas_call(block_kernel, out_shape=(jax.ShapeDtypeStruct(tile, BF), j...]
    unnamed x2 -> x1, local copies, waits for them, and re-layouts: 4.65 us -> 1.46 us
where the time goes in v3:
time: 106 us
  Pallas kernels  104 us (98%)
  local copies, waits for them, and re-layouts  1.46 us (1%)
    pallas_call x1, Pallas kernels, per_device(): pl.pallas_call(block_kernel, out_shape=(jax.ShapeDtypeStruct(tile, BF), j...  100 us
    pallas_call x1, Pallas kernels, per_device(): pl.pallas_call(merge_kernel, grid=(4,), out_shape=jax.ShapeDtypeStruct(ti...  3.91 us

profile of v3, /device:TPU:1, one launch (start us, length us, event | category | flops | bytes accessed | tf_op | source)
XLA Modules:
  0.0 105.9 jit_solution(17508500231375298508)
XLA Ops:
  0.0 1.5 %copy.8.table = f32[225,16]{1,0:T(8,128)} copy(f32[225,16]{0,1:T(8,128)} %param.12) | data formatting | bytes 28800 | tf_op args[5]
  1.5 100.5 %swin_block.1 = (bf16[4,8,4,8,1024]{4,3,2,1,0:T(8,128)(2,1)}, bf16[4,8,8,1024]{3,2,1,0:T(8,128)(2,1)}) custom-call(bf16[4,8,4,8,1024]{4,3,2,1,0:T(8,128)(2,1)} %bitcast.4, bf16[24,1024]{1,0:T(8,128)(2,1)} %wq_in.1, bf16[8,1024]{1,0:T(8,128)(2,1)} %wp_in.1, bf16[4,8,1024]{2,1,0:T(8,128)(2,1)} %bitcast.5, bf16[4,8,1024]{2,1,0:T(8,128)(2,1)} %bitcast.6, ...), custom_call_target="tpu_custom_call" | custom-call | tf_op jit(solution)/shard_map/swin_block/pallas_call | solution.py:652
  101.9 3.9 %merge_borders.1 = bf16[4,8,4,8,1024]{4,3,2,1,0:T(8,128)(2,1)} custom-call(bf16[4,8,4,8,1024]{4,3,2,1,0:T(8,128)(2,1)} %get-tuple-element.7.got, bf16[4,8,8,1024]{3,2,1,0:T(8,128)(2,1)} %get-tuple-element.8.side), custom_call_target="tpu_custom_call" | custom-call | tf_op jit(solution)/shard_map/merge_borders/pallas_call | solution.py:688

commit v4 on v3

--- a/solution.py
+++ b/solution.py
@@ -10,29 +10,30 @@
 F32 = jnp.float32
 D = 1024
 FAR = -1e30
-
-PIECES = {
-    "qa": (0, 0, 0, 1024, "xyz"),
-    "qb": (0, 8, 0, 1024, "yzx"),
-    "qc": (0, 16, 0, 1024, "zxy"),
-    "p": (1, 0, 0, 1024, "xyz"),
-    "c0a": (2, 0, 0, 384, "yzx"),
-    "c0b": (2, 0, 384, 384, "zxy"),
-    "c0c": (2, 0, 768, 256, "xyz"),
-    "c1a": (2, 1, 0, 384, "yzx"),
-    "c1b": (2, 1, 384, 384, "zxy"),
-    "c1c": (2, 1, 768, 256, "xyz"),
-    "c2a": (2, 2, 0, 384, "yzx"),
-    "c2b": (2, 2, 384, 384, "zxy"),
-    "c2c": (2, 2, 768, 256, "xyz"),
-    "c3a": (2, 3, 0, 384, "yzx"),
-    "c3b": (2, 3, 384, 384, "zxy"),
-    "c3c": (2, 3, 768, 256, "xyz"),
-}
-NAMES = list(PIECES)
-FINE = ("qa", "qb", "qc")
-COUNT = {n: 27 if n in FINE else 15 for n in NAMES}
-START = {n: sum(COUNT[m] for m in NAMES[:k]) for k, n in enumerate(NAMES)}
+TOGETHER = 4
+
+PIECES = (
+    (0, 0, 0, 1024, "xyz"),
+    (0, 8, 0, 1024, "yzx"),
+    (0, 16, 0, 1024, "xzy"),
+    (1, 0, 0, 1024, "yxz"),
+    (2, 0, 0, 512, "zxy"),
+    (2, 0, 512, 256, "xyz"),
+    (2, 0, 768, 256, "xyz"),
+    (2, 1, 0, 256, "yzx"),
+    (2, 1, 256, 384, "yzx"),
+    (2, 1, 640, 384, "xzy"),
+    (2, 2, 0, 512, "zxy"),
+    (2, 2, 512, 256, "yxz"),
+    (2, 2, 768, 256, "yzx"),
+    (2, 3, 0, 512, "yzx"),
+    (2, 3, 512, 256, "zyx"),
+    (2, 3, 768, 256, "xzy"),
+)
+NAMES = range(len(PIECES))
+FINE = (0, 1, 2)
+COUNT = [27 if n in FINE else 15 for n in NAMES]
+START = [sum(COUNT[:n]) for n in NAMES]
 FINE_STEPS = {
     1: ((), (0, 1, 2)),
     2: ((0, 1, 2), (3, 4, 7, 8)),
@@ -53,132 +54,23 @@
     6: ((9, 10), (14,)),
     7: ((11, 12, 13, 14), ()),
 }
-PLAN = [
-    ("start", 1, "qa"),
-    ("start", 1, "qb"),
-    ("start", 1, "qc"),
-    ("start", "halo", 1),
-    ("start", "halo", 3),
-    ("start", "halo", 5),
-    ("normA", 2, "qa"),
-    ("normA", 2, "qb"),
-    ("normA", 2, "qc"),
-    ("normA", "halo", 4),
-    ("normA", "halo", 0),
-    ("normA", "halo", 2),
-    ("normA", 3, "qa"),
-    ("normA", 3, "qb"),
-    ("normA", 3, "qc"),
-    ("normA", 1, "p"),
-    ("normA", 1, "c0a"),
-    ("normA", 1, "c0b"),
-    ("normA", 1, "c0c"),
-    ("normA", 1, "c1a"),
-    ("normA", 1, "c1b"),
-    ("normA", 1, "c1c"),
-    ("normA", 1, "c2a"),
-    ("normA", 1, "c2b"),
-    ("normA", 1, "c2c"),
-    ("normA", 1, "c3a"),
-    ("normA", 1, "c3b"),
-    ("normA", 1, "c3c"),
-    ("normB", 4, "qa"),
-    ("normB", 5, "qa"),
-    ("normB", 6, "qa"),
-    ("qkv0", 4, "qb"),
-    ("qkv0", 4, "qc"),
-    ("qkv0", 2, "c0b"),
-    ("qkv0", 5, "qb"),
-    ("qkv0", 5, "qc"),
-    ("qkv0", 6, "qb"),
-    ("qkv0", 6, "qc"),
-    ("qkv0", 2, "c1b"),
-    ("qkv0", 2, "p"),
-    ("qkv0", 2, "c0a"),
-    ("qkv0", 2, "c2b"),
-    ("qkv0", 2, "c0c"),
-    ("qkv0", 2, "c1a"),
-    ("qkv0", 2, "c1c"),
-    ("qkv0", 2, "c3b"),
-    ("qkv0", 2, "c2c"),
-    ("qkv0", 2, "c2a"),
-    ("qkv0", 7, "qa"),
-    ("qkv0", 2, "c3c"),
-    ("qkv0", 2, "c3a"),
-    ("qkv0", 7, "qb"),
-    ("qkv0", 7, "qc"),
-    ("qkv0", 3, "c0b"),
-    ("qkv0", 3, "c0a"),
-    ("qkv0", 3, "c1a"),
-    ("qkv0", 3, "p"),
-    ("qkv0", 3, "c2a"),
-    ("qkv0", 3, "c1b"),
-    ("qkv0", 3, "c0c"),
-    ("qkv0", 8, "qa"),
-    ("qkv0", 3, "c1c"),
-    ("qkv0", 3, "c2b"),
-    ("qkv0", 3, "c3a"),
-    ("qkv0", 3, "c2c"),
-    ("qkv0", 4, "c0a"),
-    ("qkv0", 9, "qa"),
-    ("qkv0", 3, "c3b"),
-    ("qkv0", 3, "c3c"),
-    ("qkv0", 4, "c1a"),
-    ("qkv0", 8, "qb"),
-    ("qkv0", 8, "qc"),
-    ("qkv0", 4, "c0b"),
-    ("qkv0", 4, "p"),
-    ("qkv0", 4, "c1b"),
-    ("qkv0", 4, "c0c"),
-    ("qkv0", 9, "qb"),
-    ("qkv0", 9, "qc"),
-    ("qkv3", 5, "c0a"),
-    ("qkv3", 4, "c2a"),
-    ("att0", 5, "c0b"),
-    ("att0", 4, "c2b"),
-    ("att1", 5, "p"),
-    ("att1", 4, "c1c"),
-    ("att3", 5, "c1a"),
-    ("att3", 4, "c3a"),
-    ("att5", 5, "c1b"),
-    ("att5", 4, "c3b"),
-    ("att5", 5, "c0c"),
-    ("att5", 4, "c2c"),
-    ("att7", 6, "c0a"),
-    ("att9", 6, "c0b"),
-    ("att11", 7, "c0a"),
-    ("att12", 6, "p"),
-    ("att13", 7, "c0b"),
-    ("att14", 5, "c2a"),
-    ("proj0", 7, "p"),
-    ("proj0", 5, "c1c"),
-    ("proj0", 4, "c3c"),
-    ("proj0", 5, "c2b"),
-    ("proj1", 6, "c1a"),
-    ("proj2", 6, "c0c"),
-    ("proj2", 6, "c1b"),
-    ("proj3", 7, "c1a"),
-    ("big0", 7, "c0c"),
-    ("big0", 7, "c1b"),
-    ("big0", 5, "c2c"),
-    ("big1", 6, "c1c"),
-    ("big1", 6, "c2a"),
-    ("big1", 5, "c3a"),
-    ("big1", 5, "c3b"),
-    ("big1", 5, "c3c"),
-    ("big1", 6, "c2b"),
-    ("big1", 7, "c1c"),
-    ("big2", 7, "c2a"),
-    ("big2", 7, "c2b"),
-    ("big2", 6, "c2c"),
-    ("big2", 6, "c3c"),
-    ("big2", 6, "c3a"),
-    ("big2", 6, "c3b"),
-    ("big2", 7, "c2c"),
-    ("big3", 7, "c3a"),
-    ("big3", 7, "c3b"),
-    ("big3", 7, "c3c"),
-]
+BEGIN, KEYS, BIAS, NORM_OWN, NORM_OTHER, QKV, ATTEND, PROJ, FEED = 0, 1, 2, 3, 4, 10, 20, 40, 50
+
+PLAN = (
+    (0, 1, 0), (0, 1, 1), (0, 1, 2), (0, 0, 4), (0, 0, 5), (0, 1, 3), (0, 1, 4), (0, 1, 5), (0, 1, 6), (0, 1, 7),
+    (0, 1, 8), (0, 1, 9), (0, 1, 10), (0, 1, 11), (0, 1, 12), (0, 1, 13), (0, 1, 14), (0, 1, 15), (3, 2, 0), (3, 2, 1),
+    (3, 2, 4), (3, 2, 2), (3, 0, 0), (3, 0, 2), (3, 0, 3), (3, 2, 10), (3, 2, 14), (3, 2, 3), (3, 2, 7), (3, 2, 8),
+    (4, 2, 11), (4, 2, 12), (4, 3, 1), (4, 2, 13), (4, 3, 0), (4, 3, 2), (4, 2, 5), (4, 2, 6), (4, 3, 7), (4, 2, 9),
+    (4, 3, 8), (4, 2, 15), (4, 3, 12), (4, 4, 1), (4, 5, 1), (4, 3, 4), (4, 3, 13), (4, 3, 10), (4, 3, 14), (4, 4, 0),
+    (4, 5, 0), (4, 3, 3), (4, 6, 0), (4, 3, 11), (4, 4, 2), (4, 0, 1), (4, 5, 2), (4, 6, 2), (4, 3, 9), (4, 3, 5),
+    (4, 6, 1), (4, 3, 6), (4, 3, 15), (4, 7, 1), (4, 7, 2), (4, 7, 0), (4, 4, 7), (4, 4, 8), (4, 4, 4), (4, 4, 3),
+    (10, 4, 5), (10, 4, 9), (10, 8, 0), (10, 8, 1), (10, 8, 2), (10, 9, 0), (10, 9, 1), (10, 9, 2), (11, 5, 7), (11, 4, 12),
+    (12, 5, 3), (12, 5, 4), (12, 4, 6), (12, 4, 10), (13, 5, 8), (13, 4, 13), (20, 5, 5), (20, 6, 7), (20, 4, 11), (21, 5, 9),
+    (21, 4, 15), (23, 5, 12), (23, 4, 14), (24, 6, 3), (24, 7, 7), (26, 6, 4), (27, 6, 8), (28, 7, 3), (29, 5, 6), (30, 7, 4),
+    (30, 7, 8), (31, 6, 5), (34, 7, 5), (40, 5, 10), (40, 5, 11), (41, 5, 13), (42, 6, 6), (42, 6, 9), (42, 6, 12), (50, 7, 6),
+    (50, 7, 9), (50, 7, 12), (50, 5, 14), (50, 5, 15), (50, 6, 11), (51, 6, 10), (51, 7, 11), (51, 6, 13), (52, 7, 10), (52, 7, 13),
+    (52, 6, 14), (52, 6, 15), (53, 7, 14), (53, 7, 15),
+)
 
 
 def planned(slot):
@@ -293,18 +185,18 @@
 
     def pump(slot):
         for what, name in planned(slot):
-            if what == "halo":
+            if what == 0:
                 for b in (0, 2, 1, 3):
                     halo(b, name).start()
             else:
                 step(what, name)
 
-    def pump_at(prefix, i, count):
+    def pump_at(base, i, count, together=1):
         for k in range(count):
-            if planned(f"{prefix}{k}"):
-                @pl.when(i == (k - k % 2 if prefix == "att" else k))
+            if planned(base + k):
+                @pl.when(i == k // together)
                 def _(k=k):
-                    pump(f"{prefix}{k}")
+                    pump(base + k)
 
     def geometry(b):
         ahead = b < 2
@@ -374,9 +266,9 @@
 
     for which in range(4):
         own(which).wait()
-    pump("start")
-
-    pump("keys")
+    pump(BEGIN)
+
+    pump(KEYS)
     spot = lax.broadcasted_iota(jnp.int32, (256, 512), 1)
     spot_col = spot % 8
     spot_window = spot // 128
@@ -397,7 +289,7 @@
         for w in range(4):
             keys[4 * b + w : 4 * b + w + 1] = closed[:, 128 * w : 128 * w + 128]
 
-    pump("bias")
+    pump(BIAS)
     lane = lax.broadcasted_iota(jnp.int32, (16, 256), 1)
     head_row = lax.broadcasted_iota(jnp.int32, (16, 256), 0)
     lane_row = (lane % 64) // 8
@@ -459,19 +351,19 @@
 
         lax.fori_loop(0, 16, norm_one, 0)
 
-    pump("normA")
+    pump(NORM_OWN)
     for b in range(4):
         local_tokens(b).wait()
         halo(b, 4).wait_recv()
     norm_half(0)
-    pump("normB")
+    pump(NORM_OTHER)
     for b in range(4):
         for k in (0, 1, 2, 3, 5):
             halo(b, k).wait_recv()
     norm_half(1)
 
     def qkv_one(i, _):
-        pump_at("qkv", i, 4)
+        pump_at(QKV, i, 4)
         w = wq[i // 2, pl.ds((i % 2) * 2, 2)].reshape(768, D)
         got = lax.dot_general(normed[...], w, (((1,), (1,)), ((), ())), preferred_element_type=F32)
         qkv[:, pl.ds(pl.multiple_of(i * 768, 768), 768)] = got.astype(BF)
@@ -496,7 +388,7 @@
         wide = v.astype(F32)
         return jnp.concatenate([jnp.where(p, wide, 0.0).astype(BF) for p in pick], axis=0)
 
-    def attend_one(i, _):
+    def attend_one(i):
         owned, foreign = own_row(i // 4, i % 4), other_row(i // 4, i % 4)
         top = pl.ds(pl.multiple_of(jnp.where(i < 8, owned, foreign), 32), 32)
         low = pl.ds(pl.multiple_of(jnp.where(i < 8, foreign, owned), 32), 32)
@@ -524,37 +416,36 @@
             context = jnp.dot(e, spread_heads(v), preferred_element_type=F32) / total
             att[top, pl.ds(256 * g, 256)] = context[:32].astype(BF)
             att[low, pl.ds(256 * g, 256)] = context[32:].astype(BF)
+
+    def attend_some(i, _):
+        pump_at(ATTEND, i, 16, TOGETHER)
+        for u in range(TOGETHER):
+            attend_one(i * TOGETHER + u)
         return 0
 
-    def attend_two(i, _):
-        pump_at("att", i * 2, 16)
-        attend_one(i * 2, 0)
-        attend_one(i * 2 + 1, 0)
-        return 0
-
-    lax.fori_loop(0, 8, attend_two, 0)
+    lax.fori_loop(0, 16 // TOGETHER, attend_some, 0)
 
     def proj_one(i, _):
-        pump_at("proj", i, 4)
-        rows = pl.ds(pl.multiple_of(i * 256, 256), 256)
+        pump_at(PROJ, i, 4, 2)
+        rows = pl.ds(pl.multiple_of(i * 512, 512), 512)
         got = lax.dot_general(
             att[rows], wp[...].reshape(D, D), (((1,), (1,)), ((), ())), preferred_element_type=F32
         )
-        for w in range(8):
-            part = pl.ds(pl.multiple_of(i * 256 + w * 32, 32), 32)
-            slot = i * 8 + w
+        for w in range(16):
+            part = pl.ds(pl.multiple_of(i * 512 + w * 32, 32), 32)
+            slot = i * 16 + w
             edge_b = jnp.clip(slot - 12, 0, 3)
             inner_b = jnp.minimum(slot // 3, 3)
             b = jnp.where(slot < 12, inner_b, jnp.where(slot < 16, edge_b, (slot // 4 + 2 * core) % 4))
             inner_w = jnp.minimum(slot % 3 + inner_b % 2, 3)
             at_w = jnp.where(slot < 12, inner_w, jnp.where(slot < 16, 3 - 3 * (edge_b % 2), slot % 4))
-            before = window_half(b, at_w, i // 2)
+            before = window_half(b, at_w, i)
             whole = (before + got[32 * w : 32 * w + 32]).astype(BF)
             acc[part] = whole.astype(F32)
             normed[part] = layer_norm(whole.astype(F32))
         return 0
 
-    lax.fori_loop(0, 4, proj_one, 0)
+    lax.fori_loop(0, 2, proj_one, 0)
 
     def feed(rows, k):
         up = wf[:, :, :, :, :, k, pl.ds(0, 8)].reshape(D, D)
@@ -564,7 +455,7 @@
         acc[rows] += jnp.dot(hidden, down, preferred_element_type=F32)
 
     def feed_sent(k, _):
-        pump_at("big", k, 3)
+        pump_at(FEED, k, 3)
         feed(pl.ds(384, 640), k)
         return 0
 
@@ -584,7 +475,7 @@
             returns(b, 2).start()
 
     lax.fori_loop(0, 3, feed_sent, 0)
-    pump("big3")
+    pump(FEED + 3)
     feed(pl.ds(768, 256), 3)
     pl.when(core == 1)(lambda: finish_other((0, 1)))
     pl.when(core == 0)(lambda: finish_other((2, 3)))
@@ -625,21 +516,30 @@
             returns(b, k).wait_send()
 
 
-def merge_kernel(got, side, out):
-    out[...] = got[...]
+def merge_kernel(got, side, out, held, halves, in_sem, side_sem, out_sem):
     late = lax.broadcasted_iota(jnp.int32, (64, D), 0) % 8 >= 4
-    from_side = side[...].astype(F32).reshape(64, D)
-    odd = pl.program_id(0) % 2 == 1
-
-    @pl.when(jnp.logical_not(odd))
-    def _():
-        here = got[0, :, 0].astype(F32).reshape(64, D)
-        out[0, :, 0] = jnp.where(late, here, from_side).astype(BF).reshape(8, 8, D)
-
-    @pl.when(odd)
-    def _():
-        here = got[0, :, 3].astype(F32).reshape(64, D)
-        out[0, :, 3] = jnp.where(late, from_side, here).astype(BF).reshape(8, 8, D)
+
+    def moves(b):
+        return (
+            pltpu.make_async_copy(side.at[b], halves.at[b], side_sem.at[b]),
+            pltpu.make_async_copy(got.at[b], held.at[b], in_sem.at[b]),
+            pltpu.make_async_copy(held.at[b], out.at[b], out_sem.at[b]),
+        )
+
+    for b in range(4):
+        moves(b)[0].start()
+        moves(b)[1].start()
+    for b in range(4):
+        moves(b)[0].wait()
+        moves(b)[1].wait()
+        border = 0 if b % 2 == 0 else 3
+        here = held[b, :, border].astype(F32).reshape(64, D)
+        there = halves[b].astype(F32).reshape(64, D)
+        both = jnp.where(late, here, there) if b % 2 == 0 else jnp.where(late, there, here)
+        held[b, :, border] = both.astype(BF).reshape(8, 8, D)
+        moves(b)[2].start()
+    for b in range(4):
+        moves(b)[2].wait()
 
 
 def per_device(tokens, qkv_weight, proj_weight, up_weight, down_weight, bias_table, sea_mask):
@@ -647,7 +547,7 @@
     vmem = pl.BlockSpec(memory_space=pltpu.VMEM)
     shard = (2, 4, 2, 2, 4)
     tile = (4, 8, 4, 8, D)
-    messages = sum(COUNT.values())
+    messages = sum(COUNT)
     dma = pltpu.SemaphoreType.DMA
     got, side = pl.pallas_call(
         block_kernel,
@@ -687,13 +587,16 @@
     )
     out = pl.pallas_call(
         merge_kernel,
-        grid=(4,),
         out_shape=jax.ShapeDtypeStruct(tile, BF),
-        in_specs=[
-            pl.BlockSpec((1, 8, 4, 8, D), lambda b: (b, 0, 0, 0, 0)),
-            pl.BlockSpec((1, 8, 8, D), lambda b: (b, 0, 0, 0)),
+        in_specs=[hbm, hbm],
+        out_specs=hbm,
+        scratch_shapes=[
+            pltpu.VMEM(tile, BF),
+            pltpu.VMEM((4, 8, 8, D), BF),
+            dma((4,)),
+            dma((4,)),
+            dma((4,)),
         ],
-        out_specs=pl.BlockSpec((1, 8, 4, 8, D), lambda b: (b, 0, 0, 0, 0)),
         name="merge_borders",
     )(got, side)
     return out.reshape(tokens.shape)

time: 106 us -> 104 us (0.981)
  Pallas kernels: 104 us -> 102 us
    pallas_call x1, Pallas kernels: 3.91 us -> 2.64 us  [per_device(): pl.pallas_call(merge_kernel, out_shape=jax.ShapeDtypeStruct(tile, BF), in...]
where the time goes in v4:
time: 104 us
  Pallas kernels  102 us (98%)
  local copies, waits for them, and re-layouts  1.46 us (1%)
    pallas_call x1, Pallas kernels, per_device(): pl.pallas_call(block_kernel, out_shape=(jax.ShapeDtypeStruct(tile, BF), j...  99.5 us
    pallas_call x1, Pallas kernels, per_device(): pl.pallas_call(merge_kernel, out_shape=jax.ShapeDtypeStruct(tile, BF), in...  2.64 us

profile of v4, /device:TPU:1, one launch (start us, length us, event | category | flops | bytes accessed | tf_op | source)
XLA Modules:
  0.0 103.8 jit_solution(13405357862306519650)
XLA Ops:
  0.0 1.5 %copy.8.table = f32[225,16]{1,0:T(8,128)} copy(f32[225,16]{0,1:T(8,128)} %param.12) | data formatting | bytes 28800 | tf_op args[5]
  1.5 99.5 %swin_block.1 = (bf16[4,8,4,8,1024]{4,3,2,1,0:T(8,128)(2,1)}, bf16[4,8,8,1024]{3,2,1,0:T(8,128)(2,1)}) custom-call(bf16[4,8,4,8,1024]{4,3,2,1,0:T(8,128)(2,1)} %bitcast.4, bf16[24,1024]{1,0:T(8,128)(2,1)} %wq_in.1, bf16[8,1024]{1,0:T(8,128)(2,1)} %wp_in.1, bf16[4,8,1024]{2,1,0:T(8,128)(2,1)} %bitcast.5, bf16[4,8,1024]{2,1,0:T(8,128)(2,1)} %bitcast.6, ...), custom_call_target="tpu_custom_call" | custom-call | tf_op jit(solution)/shard_map/swin_block/pallas_call | solution.py:552
  101.0 2.6 %merge_borders.1 = bf16[4,8,4,8,1024]{4,3,2,1,0:T(8,128)(2,1)} custom-call(bf16[4,8,4,8,1024]{4,3,2,1,0:T(8,128)(2,1)} %get-tuple-element.7.got, bf16[4,8,8,1024]{3,2,1,0:T(8,128)(2,1)} %get-tuple-element.8.side), custom_call_target="tpu_custom_call" | custom-call | tf_op jit(solution)/shard_map/merge_borders/pallas_call | solution.py:588
